TPU v7x, 32 devices: a whole 2x2x4 slice. The times are simulated.
32 devices in a mesh: inner: 4 (over z), outer: 8 (over y, x, core).
Axes of the slice: x: 2, y: 2, z: 4, core: 2. Of those that a mesh axis runs over, the one named last changes fastest.
Arguments:
- inner_state: float32 [2, 16, 2048], P(None, 'inner', 'outer'), may hold values from -6 to 6
- outer_state: float32 [2, 640, 4096], P(None, 'inner', 'outer'), may hold values from -6 to 6
- energies: float32 [16, 2048], P('inner', 'outer'), may hold values from -2 to 2
- dipole: float32 [16, 2048, 2048], P('inner', 'outer'), may hold values from -0.125 to 0.125
- surface: float32 [16, 40, 2048], P('inner', None, 'outer'), may hold values from -0.125 to 0.125
- thresholds: float32 [640], P('inner'), may hold values from 0 to 2
- coupling_coef: float32 [16, 40, 40], P('inner'), may hold values from -1 to 1
- coupling_pattern: int32 [16, 40, 40], P('inner'), may hold values 0 or 1
- block_sizes: int32 [16], P('inner'), may hold values from 1 to 2048, 30720 in all
- field_strength: float32 [2], replicated, may hold values from 0.5 to 2
Outputs:
- inner_final: float32 [2, 16, 2048], P(None, 'inner', 'outer')
- outer_final: float32 [2, 640, 4096], P(None, 'inner', 'outer')
All inputs are finite; a program needn't handle non-finite values. No bound on the sum of `coupling_pattern` or of `block_sizes` on one device may be relied on, other than what follows from the above.
Results may differ from a plain program's by a relative error of at most 0.0001.
Values sent between devices are 32-bit elements; how exact they have to be, the bound alone decides.
A program may use at most 128 MiB of HBM per device.

v0:
```python
import jax
import jax.numpy as jnp
from jax import lax
from jax.sharding import PartitionSpec as P

STEPS = 2
ORDER = 4
kinetic_scale = 3.125
time_step = 0.1


def from_behind(block, axis, distance):
    devices = range(lax.axis_size(axis))
    route = [(i - distance, i) for i in devices if i - distance in devices]
    return lax.ppermute(block, axis, route)


def spread(shard, axis, root):
    mine = lax.axis_index(axis) == root
    return lax.psum(jnp.where(mine, shard, jnp.zeros_like(shard)), axis)


def with_halo(cells, sides, width):
    for axis, dim in sides:
        count = lax.axis_size(axis)
        ends = count - 1
        head = lax.slice_in_dim(cells, 0, width, axis=dim)
        tail = lax.slice_in_dim(cells, cells.shape[dim] - width, cells.shape[dim], axis=dim)
        cells = jnp.concatenate(
            [
                lax.ppermute(tail, axis, [(i, (i + 1) % count) for i in range(ends)]),
                cells,
                lax.ppermute(head, axis, [((i + 1) % count, i) for i in range(ends)]),
            ],
            axis=dim,
        )
    return cells


def reduce_partials(partial_terms, partial_boundary):
    own_terms = lax.psum_scatter(partial_terms, "outer", scatter_dimension=2, tiled=True)
    boundary = lax.psum(partial_boundary, "outer")
    return (own_terms, boundary)


def local(
    inner_state,
    outer_state,
    energies,
    dipole,
    surface,
    thresholds,
    coupling_coef,
    coupling_pattern,
    block_sizes,
    field_strength,
):
    highest = lax.Precision.HIGHEST
    blocks = dipole.shape[0]
    row_count = dipole.shape[1]
    channels = coupling_coef.shape[1]
    radial = outer_state.shape[2]
    sector_index = lax.axis_index("outer")
    row_index = sector_index * row_count + jnp.arange(row_count, dtype=jnp.int32)
    live_rows = (row_index[None, :] < block_sizes[:, None]).astype(jnp.float32)
    coupling = coupling_coef * coupling_pattern.astype(jnp.float32)
    first_sector = jnp.where(sector_index == 0, 1.0, 0.0).astype(jnp.float32)
    edge_mask = first_sector * (jnp.arange(radial, dtype=jnp.int32) == 0).astype(jnp.float32)
    prev_dipole, prev_coupling = from_behind((dipole[blocks - 1], coupling[blocks - 1]), "inner", 1)
    current = (inner_state * live_rows, outer_state)
    for time_index in range(STEPS):
        strength = field_strength[time_index]
        taylor_term = current
        accumulated = current
        for power in range(1, ORDER + 1):
            inner_part = taylor_term[0]
            outer_part = taylor_term[1]
            channel_grid = outer_part.reshape(2, blocks, channels, radial)
            next_first, next_channels = from_behind(
                (inner_part[:, 0], channel_grid[:, 0]), "inner", -1
            )
            extended = jnp.concatenate([inner_part, next_first[:, None]], axis=1)
            gathered = lax.all_gather(extended, "outer", axis=2, tiled=True)
            edge_values = spread(outer_part[:, :, 0], "outer", 0)
            forward = jnp.einsum("lij,plj->pli", dipole, gathered[:, 1:], precision=highest)
            grid_next = jnp.concatenate([channel_grid[:, 1:], next_channels[:, None]], axis=1)
            upward = jnp.einsum("lab,plbr->plar", coupling, grid_next, precision=highest)
            partial_boundary = jnp.einsum("lcs,pls->plc", surface, inner_part, precision=highest)
            prev_rows, prev_channels = from_behind(
                (inner_part[:, blocks - 1], channel_grid[:, blocks - 1]), "inner", 1
            )
            source_rows = jnp.concatenate([prev_rows[:, None], inner_part[:, : blocks - 1]], axis=1)
            source_blocks = jnp.concatenate([prev_dipole[None], dipole[: blocks - 1]], axis=0)
            partial_terms = jnp.einsum(
                "lji,plj->pli", source_blocks, source_rows, precision=highest
            )
            backward, boundary = reduce_partials(partial_terms, partial_boundary)
            source_grid = jnp.concatenate(
                [prev_channels[:, None], channel_grid[:, : blocks - 1]], axis=1
            )
            source_coupling = jnp.concatenate([prev_coupling[None], coupling[: blocks - 1]], axis=0)
            downward = jnp.einsum("lba,plbr->plar", source_coupling, source_grid, precision=highest)
            first_point = edge_values.reshape(2, blocks, channels)
            surf_term = jnp.einsum("lcs,plc->pls", surface, first_point, precision=highest)
            inner_image = live_rows * (
                energies * inner_part + strength * (forward + backward) - kinetic_scale * surf_term
            )
            padded = with_halo(outer_part, (("outer", 2),), 1)
            left_cells = (
                padded[:, :, :radial]
                + edge_mask[None, None, :] * boundary.reshape(2, blocks * channels)[:, :, None]
            )
            right_cells = padded[:, :, 2:]
            kinetic = kinetic_scale * (2.0 * outer_part - left_cells - right_cells)
            outer_image = (
                kinetic
                + thresholds[None, :, None] * outer_part
                + strength * (upward + downward).reshape(2, blocks * channels, radial)
            )
            inner_image, outer_image = (inner_image, outer_image)
            factor = time_step / power
            taylor_term = (
                factor * jnp.stack([inner_image[1], -inner_image[0]]),
                factor * jnp.stack([outer_image[1], -outer_image[0]]),
            )
            accumulated = (accumulated[0] + taylor_term[0], accumulated[1] + taylor_term[1])
        current = accumulated
    return (current[0], current[1])


def solution(mesh):
    placed = (
        P(None, "inner", "outer"),
        P(None, "inner", "outer"),
        P("inner", "outer"),
        P("inner", "outer", None),
        P("inner", None, "outer"),
        P("inner"),
        P("inner", None, None),
        P("inner", None, None),
        P("inner"),
        P(),
    )
    return jax.shard_map(
        local,
        mesh=mesh,
        in_specs=placed,
        out_specs=(P(None, "inner", "outer"), P(None, "inner", "outer")),
        check_vma=False,
    )
```

profile of v0, /device:TPU:12, one launch (start us, length us, event | category | flops | bytes accessed | tf_op | source)
XLA Modules:
  0.0 834.8 jit_solution(18084127534141652575)
XLA Ops:
  8.7 3.5 collective-permute-start.1
  15.4 3.5 collective-permute-start.2
  34.9 12.6 %all-reduce.7 = (f32[2,160]{1,0:T(2,128)}, f32[2,4,40]{2,0,1:T(2,128)S(1)}) all-reduce(f32[2,160]{1,0:T(2,128)S(1)} %mul.616, f32[2,4,40]{2,0,1:T(2,128)S(1)} %copy.69), channel_id=1, replica_groups=mesh['inner'=4,'outer'=8] {'outer'}, use_global_device_ids=true, to_apply=%region_3.4 | all-reduce | flops 640 | bytes 5120 | tf_op jit(solution)/shard_map/psum | solution.py:42
  48.9 6.3 slice.446
  55.2 4.7 collective-permute-start.7
  59.9 8.3 all_gather.24
  70.5 4.2 collective-permute-start.6
  84.6 3.9 collective-permute-start.14
  91.3 4.5 collective-permute-start.13
  97.4 7.4 convolution_bitcast_fusion.7
  104.9 4.2 copy.137
  109.1 4.5 reshape.173
  117.4 30.5 %reduce-scatter.25.cloned.1.call-done = f32[256,8]{1,0:T(8,128)} async-done(((f32[2048,8]{1,0:T(8,128)}), f32[256,8]{1,0:T(8,128)}) %reduce-scatter.25.cloned.1.call-update) | async-done | bytes 8208
  151.2 9.8 %fusion.55 = f32[2,4,256]{2,0,1:T(2,128)S(1)} fusion(f32[2,4,256]{2,0,1:T(2,128)S(1)} %fusion.63, f32[2,4,256]{2,0,1:T(2,128)S(1)} %copy.138, f32[2,5,2048]{2,0,1:T(2,128)S(1)} %all_gather.24, f32[4,256,2048]{2,1,0:T(8,128)} %param.13, f32[2,4,256]{2,0,1:T(2,128)S(1)} %copy-done.49, f32[]{:T(128)} %bitcast, f32[4,256]{1,0:T(4,128)S(1)} %copy-done.53, ...), kind=kOutput, calls=%fused_computation.81 | convolution fusion | flops 50343936 | bytes 8511492 | tf_op jit(solution)/shard_map/lij,plj->pli/dot_general | solution.py:85
  161.4 12.6 %all-reduce.6 = (f32[2,160]{1,0:T(2,128)S(1)}, f32[2,4,40]{2,0,1:T(2,128)S(1)}) all-reduce(f32[2,160]{1,0:T(2,128)S(1)} %mul.639, f32[2,4,40]{2,0,1:T(2,128)S(1)} %copy.79), channel_id=1, replica_groups=mesh['inner'=4,'outer'=8] {'outer'}, use_global_device_ids=true, to_apply=%region_6.7 | all-reduce | flops 640 | bytes 5120 | tf_op jit(solution)/shard_map/psum | solution.py:42
  194.4 4.5 collective-permute-start.19
  199.0 6.8 convolution_bitcast_fusion.6
  209.0 4.5 reshape.175
  213.6 7.7 all_gather.25
  221.3 28.3 %reduce-scatter.27.cloned.1.call-done = f32[256,8]{1,0:T(8,128)} async-done(((f32[2048,8]{1,0:T(8,128)}), f32[256,8]{1,0:T(8,128)}) %reduce-scatter.27.cloned.1.call-update) | async-done | bytes 8208
  252.8 9.8 %fusion.50 = f32[2,4,256]{2,0,1:T(2,128)S(1)} fusion(f32[2,4,256]{2,0,1:T(2,128)S(1)} %fusion.62, f32[2,4,256]{2,0,1:T(2,128)S(1)} %copy.140, f32[2,5,2048]{2,0,1:T(2,128)S(1)} %all_gather.25, f32[4,256,2048]{2,1,0:T(8,128)} %param.13, f32[4,256]{1,0:T(4,128)S(1)} %get-tuple-element.129, f32[]{:T(128)} %bitcast, f32[4,256]{1,0:T(4,128)S(1)} %compare_convert_fusion, ...), kind=kOutput, calls=%fused_computation.75 | convolution fusion | flops 50345984 | bytes 8511492 | tf_op jit(solution)/shard_map/lij,plj->pli/dot_general | solution.py:85
  266.4 12.8 %all-reduce.5 = (f32[2,160]{1,0:T(2,128)}, f32[2,4,40]{2,0,1:T(2,128)S(1)}) all-reduce(f32[2,160]{1,0:T(2,128)S(1)} %mul.662, f32[2,4,40]{2,0,1:T(2,128)S(1)} %copy.83), channel_id=1, replica_groups=mesh['inner'=4,'outer'=8] {'outer'}, use_global_device_ids=true, to_apply=%region_9.10 | all-reduce | flops 640 | bytes 5120 | tf_op jit(solution)/shard_map/psum | solution.py:42
  282.0 6.8 convolution_bitcast_fusion.5
  292.0 4.5 reshape.177
  296.6 8.4 %all_gather.26 = f32[2,5,2048]{2,0,1:T(2,128)S(1)} all-gather(f32[2,5,256]{2,0,1:T(2,128)S(1)} %pad_maximum_fusion.25), channel_id=1, replica_groups=mesh['inner'=4,'outer'=8] {'outer'}, dimensions={2}, use_global_device_ids=true | all-gather | bytes 92160 | tf_op jit(solution)/shard_map/all_gather | solution.py:83
  315.8 3.4 collective-permute-start.27
  324.2 4.5 collective-permute-start.25
  328.8 4.2 reduce-scatter.29.cloned.1.call-done
  336.2 9.8 %fusion.45 = f32[2,4,256]{2,0,1:T(2,128)S(1)} fusion(f32[2,4,256]{2,0,1:T(2,128)S(1)} %fusion.61, f32[2,4,256]{2,0,1:T(2,128)S(1)} %copy.142, f32[2,5,2048]{2,0,1:T(2,128)S(1)} %all_gather.26, f32[4,256,2048]{2,1,0:T(8,128)} %param.13, f32[4,256]{1,0:T(4,128)S(1)} %get-tuple-element.130, f32[]{:T(128)} %bitcast, f32[4,256]{1,0:T(4,128)S(1)} %compare_convert_fusion, ...), kind=kOutput, calls=%fused_computation.69 | convolution fusion | flops 50345984 | bytes 8511492 | tf_op jit(solution)/shard_map/lij,plj->pli/dot_general | solution.py:85
  346.3 3.7 collective-permute-start.17
  350.1 12.7 %all-reduce.4 = (f32[2,160]{1,0:T(2,128)}, f32[2,4,40]{2,0,1:T(2,128)S(1)}) all-reduce(f32[2,160]{1,0:T(2,128)S(1)} %mul.684, f32[2,4,40]{2,0,1:T(2,128)} %copy.87), channel_id=1, replica_groups=mesh['inner'=4,'outer'=8] {'outer'}, use_global_device_ids=true, to_apply=%region_12.13 | all-reduce | flops 640 | bytes 5120 | tf_op jit(solution)/shard_map/psum | solution.py:42
  365.9 6.8 convolution_bitcast_fusion.4
  375.9 4.5 reshape.179
  380.6 8.0 all_gather.27
  388.6 28.1 %reduce-scatter.31.cloned.1.call-done = f32[256,8]{1,0:T(8,128)} async-done(((f32[2048,8]{1,0:T(8,128)}), f32[256,8]{1,0:T(8,128)}) %reduce-scatter.31.cloned.1.call-update) | async-done | bytes 8208
  419.8 9.8 %fusion.40 = f32[2,4,256]{2,0,1:T(2,128)S(1)} fusion(f32[2,4,256]{2,0,1:T(2,128)} %fusion.60, f32[2,4,256]{2,0,1:T(2,128)S(1)} %copy.144, f32[2,5,2048]{2,0,1:T(2,128)S(1)} %all_gather.27, f32[4,256,2048]{2,1,0:T(8,128)} %param.13, f32[4,256]{1,0:T(4,128)S(1)} %get-tuple-element.128, f32[]{:T(128)} %bitcast, f32[4,256]{1,0:T(4,128)S(1)} %compare_convert_fusion, ...), kind=kOutput, calls=%fused_computation.63 | convolution fusion | flops 50345984 | bytes 8511492 | tf_op jit(solution)/shard_map/lij,plj->pli/dot_general | solution.py:85
  438.0 6.8 convolution_bitcast_fusion.3
  448.6 4.5 reshape.181
  453.2 8.3 all_gather.28
  472.7 14.2 %all-reduce.3 = (f32[2,160]{1,0:T(2,128)}, f32[2,4,40]{2,0,1:T(2,128)}) all-reduce(f32[2,160]{1,0:T(2,128)} %mul.704, f32[2,4,40]{2,0,1:T(2,128)S(1)} %copy.91), channel_id=1, replica_groups=mesh['inner'=4,'outer'=8] {'outer'}, use_global_device_ids=true, to_apply=%region_15.16 | all-reduce | flops 640 | bytes 5120 | tf_op jit(solution)/shard_map/psum | solution.py:42
  488.4 3.8 collective-permute-start.33
  496.8 4.9 collective-permute-start.31
  505.6 9.8 %fusion.35 = f32[2,4,256]{2,0,1:T(2,128)S(1)} fusion(f32[2,4,256]{2,0,1:T(2,128)} %fusion.59, f32[2,4,256]{2,0,1:T(2,128)} %copy.146, f32[2,5,2048]{2,0,1:T(2,128)S(1)} %all_gather.28, f32[4,256,2048]{2,1,0:T(8,128)} %param.13, f32[2,4,256]{2,0,1:T(2,128)S(1)} %fusion.196, f32[]{:T(128)} %bitcast.65, f32[4,256]{1,0:T(4,128)S(1)} %copy-done.53, ...), kind=kOutput, calls=%fused_computation.57 | convolution fusion | flops 50343936 | bytes 8511492 | tf_op jit(solution)/shard_map/lij,plj->pli/dot_general | solution.py:85
  523.5 6.8 convolution_bitcast_fusion.2
  533.5 4.5 reshape.183
  538.8 7.5 all_gather.29
  557.7 14.5 %all-reduce.2 = (f32[2,160]{1,0:T(2,128)}, f32[2,4,40]{2,0,1:T(2,128)}) all-reduce(f32[2,160]{1,0:T(2,128)} %mul.721, f32[2,4,40]{2,0,1:T(2,128)S(1)} %copy.99), channel_id=1, replica_groups=mesh['inner'=4,'outer'=8] {'outer'}, use_global_device_ids=true, to_apply=%region_18.19 | all-reduce | flops 640 | bytes 5120 | tf_op jit(solution)/shard_map/psum | solution.py:42
  573.7 3.9 collective-permute-start.39
  582.1 4.5 collective-permute-start.37
  590.5 9.8 %fusion.30 = f32[2,4,256]{2,0,1:T(2,128)S(1)} fusion(f32[2,4,256]{2,0,1:T(2,128)} %fusion.58, f32[2,4,256]{2,0,1:T(2,128)} %copy.148, f32[2,5,2048]{2,0,1:T(2,128)S(1)} %all_gather.29, f32[4,256,2048]{2,1,0:T(8,128)} %param.13, f32[]{:T(128)} %bitcast.65, f32[4,256]{1,0:T(4,128)S(1)} %copy-done.55, f32[4,256]{1,0:T(4,128)S(1)} %compare_convert_fusion, ...), kind=kOutput, calls=%fused_computation.51 | convolution fusion | flops 50345984 | bytes 8511492 | tf_op jit(solution)/shard_map/lij,plj->pli/dot_general | solution.py:85
  608.4 6.8 convolution_bitcast_fusion.1
  618.4 4.5 reshape.185
  623.7 7.7 all_gather.30
  631.3 28.7 %reduce-scatter.37.cloned.1.call-done = f32[256,8]{1,0:T(8,128)} async-done(((f32[2048,8]{1,0:T(8,128)}), f32[256,8]{1,0:T(8,128)}) %reduce-scatter.37.cloned.1.call-update) | async-done | bytes 8208
  677.2 13.2 %all-reduce.1 = (f32[2,160]{1,0:T(2,128)}, f32[2,4,40]{2,0,1:T(2,128)}) all-reduce(f32[2,160]{1,0:T(2,128)} %mul.738, f32[2,4,40]{2,0,1:T(2,128)} %copy.103), channel_id=1, replica_groups=mesh['inner'=4,'outer'=8] {'outer'}, use_global_device_ids=true, to_apply=%region_21.22 | all-reduce | flops 640 | bytes 5120 | tf_op jit(solution)/shard_map/psum | solution.py:42
  691.3 9.8 %fusion.25 = f32[2,4,256]{2,0,1:T(2,128)S(1)} fusion(f32[2,4,256]{2,0,1:T(2,128)S(1)} %fusion.57, f32[2,4,256]{2,0,1:T(2,128)} %copy.150, f32[2,5,2048]{2,0,1:T(2,128)S(1)} %all_gather.30, f32[4,256,2048]{2,1,0:T(8,128)} %param.13, f32[]{:T(128)} %bitcast.65, f32[4,256]{1,0:T(4,128)S(1)} %get-tuple-element.130, f32[4,256]{1,0:T(4,128)S(1)} %compare_convert_fusion, ...), kind=kOutput, calls=%fused_computation.45 | convolution fusion | flops 50345984 | bytes 8511492 | tf_op jit(solution)/shard_map/lij,plj->pli/dot_general | solution.py:85
  714.4 4.5 collective-permute-start.43
  721.3 6.8 convolution_bitcast_fusion
  731.3 4.6 reshape.187
  736.6 7.5 all_gather.31
  744.0 28.4 %reduce-scatter.39.cloned.1.call-done = f32[256,8]{1,0:T(8,128)} async-done(((f32[2048,8]{1,0:T(8,128)}), f32[256,8]{1,0:T(8,128)}) %reduce-scatter.39.cloned.1.call-update) | async-done | bytes 8208
  791.1 4.5 collective-permute-start.47
  795.6 13.1 %all-reduce = (f32[2,4,40]{2,0,1:T(2,128)S(1)}, f32[2,160]{1,0:T(2,128)S(1)}) all-reduce(f32[2,4,40]{2,0,1:T(2,128)S(1)} %copy.107, f32[2,160]{1,0:T(2,128)S(1)} %mul.753), channel_id=1, replica_groups=mesh['inner'=4,'outer'=8] {'outer'}, use_global_device_ids=true, to_apply=%region_22.23 | all-reduce | flops 640 | bytes 5120 | tf_op jit(solution)/shard_map/psum | solution.py:20
  809.1 10.4 %fusion.20 = f32[2,4,256]{2,0,1:T(2,128)S(1)} fusion(f32[2,4,256]{2,0,1:T(2,128)S(1)} %fusion.56, f32[2,4,256]{2,0,1:T(2,128)S(1)} %copy.152, f32[2,5,2048]{2,0,1:T(2,128)S(1)} %all_gather.31, f32[4,256,2048]{2,1,0:T(8,128)} %param.13, f32[]{:T(128)} %bitcast.65, f32[4,256]{1,0:T(4,128)S(1)} %get-tuple-element.128, f32[4,256]{1,0:T(4,128)S(1)} %compare_convert_fusion, ...), kind=kOutput, calls=%fused_computation.39 | convolution fusion | flops 50345984 | bytes 8511492 | tf_op jit(solution)/shard_map/lij,plj->pli/dot_general | solution.py:85
  (452 shorter events, 252.7 us)
Async XLA Ops:
  7.2 140.7 %reduce-scatter.25.cloned.1.call-start = ((), (), s32[]{:S(2)}) async-start(), calls=%async_computation.8 | async-start | bytes 1179648
  8.7 51.2 %copy-start.48 = (f32[2,4,256]{2,0,1:T(2,128)}, f32[2,4,256]{2,0,1:T(2,128)S(1)}, u32[]{:S(2)}) copy-start(f32[2,4,256]{2,0,1:T(2,128)S(1)} %copy_multiply_fusion) | copy-start | bytes 24580
  8.7 88.7 %collective-permute-start.1 = (f32[2,256]{1,0:T(2,128)S(1)}, f32[2,256]{1,0:T(2,128)S(1)}, u32[]{:S(2)}, u32[]{:S(2)}) collective-permute-start(f32[2,256]{1,0:T(2,128)S(1)} %get-tuple-element.127), channel_id=1, source_target_pairs={{0,8},{8,16},{16,24},{1,9},{9,17},{17,25},{2,10},{10,18},{18,26},{... | collective-permute-start | bytes 6152 | tf_op jit(solution)/shard_map/ppermute | solution.py:15
  15.4 82.0 %collective-permute-start.2 = (f32[256,2048]{1,0:T(8,128)}, f32[256,2048]{1,0:T(8,128)S(1)}, u32[]{:S(2)}, u32[]{:S(2)}) collective-permute-start(f32[256,2048]{1,0:T(8,128)} %slice_bitcast_fusion), channel_id=1, source_target_pairs={{0,8},{8,16},{16,24},{1,9},{9,17},{17,25},{2,10},{10,18},{18,26},{... | collective-permute-start | bytes 6291464 | tf_op jit(solution)/shard_map/ppermute | solution.py:15
  18.9 36.3 %collective-permute-start = (f32[2,256]{1,0:T(2,128)S(1)}, f32[2,256]{1,0:T(2,128)S(1)}, u32[]{:S(2)}, u32[]{:S(2)}) collective-permute-start(f32[2,256]{1,0:T(2,128)S(1)} %get-tuple-element.126), channel_id=1, source_target_pairs={{8,0},{16,8},{24,16},{9,1},{17,9},{25,17},{10,2},{18,10},{26,18},{... | collective-permute-start | bytes 6152 | tf_op jit(solution)/shard_map/ppermute | solution.py:15
  24.0 44.3 %collective-permute-start.9 = (f32[40,40]{0,1:T(8,128)}, f32[40,40]{0,1:T(8,128)S(1)}, u32[]{:S(2)}, u32[]{:S(2)}) collective-permute-start(f32[40,40]{0,1:T(8,128)} %slice_bitcast_fusion.17), channel_id=1, source_target_pairs={{0,8},{8,16},{16,24},{1,9},{9,17},{17,25},{2,10},{10,18},{18,26},{... | collective-permute-start | bytes 19208 | tf_op jit(solution)/shard_map/ppermute | solution.py:15
  28.4 42.2 %collective-permute-start.8 = (f32[2,40,512]{2,1,0:T(8,128)S(1)}, f32[2,40,512]{2,1,0:T(8,128)}, u32[]{:S(2)}, u32[]{:S(2)}) collective-permute-start(f32[2,40,512]{2,1,0:T(8,128)S(1)} %get-tuple-element.95), channel_id=1, source_target_pairs={{0,8},{8,16},{16,24},{1,9},{9,17},{17,25},{2,10},{10,18},{18,26},{... | collective-permute-start | bytes 491528 | tf_op jit(solution)/shard_map/ppermute | solution.py:15
  48.2 204.6 %copy-start.54 = (f32[4,256]{1,0:T(4,128)}, f32[4,256]{1,0:T(4,128)S(1)}, u32[]{:S(2)}) copy-start(f32[4,256]{1,0:T(4,128)S(1)} %get-tuple-element.129) | copy-start | bytes 12292
  55.2 21.2 %collective-permute-start.7 = (f32[2,40,512]{2,1,0:T(8,128)S(1)}, f32[2,40,512]{2,1,0:T(8,128)S(1)}, u32[]{:S(2)}, u32[]{:S(2)}) collective-permute-start(f32[2,40,512]{2,1,0:T(8,128)S(1)} %get-tuple-element.94), channel_id=1, source_target_pairs={{8,0},{16,8},{24,16},{9,1},{17,9},{25,17},{10,2},{18,10},{26,18},{... | collective-permute-start | bytes 491528 | tf_op jit(solution)/shard_map/ppermute | solution.py:15
  68.3 9.5 %collective-permute-start.5 = (f32[2,160,1]{2,1,0:T(8,128)S(1)}, f32[2,160,1]{2,1,0:T(8,128)S(1)}, u32[]{:S(2)}, u32[]{:S(2)}) collective-permute-start(f32[2,160,1]{2,1,0:T(8,128)S(1)} %copy-done.51), channel_id=1, source_target_pairs={{0,1},{1,2},{2,3},{3,4},{4,5},{5,6},{6,7},{8,9},{9,10},{10,11},{11... | collective-permute-start | bytes 3848 | tf_op jit(solution)/shard_map/ppermute | solution.py:31
  70.5 7.2 collective-permute-start.6
  82.6 8.7 %collective-permute-start.15 = (f32[2,40,512]{2,1,0:T(8,128)S(1)}, f32[2,40,512]{2,1,0:T(8,128)S(1)}, u32[]{:S(2)}, u32[]{:S(2)}) collective-permute-start(f32[2,40,512]{2,1,0:T(8,128)S(1)} %get-tuple-element.86), channel_id=1, source_target_pairs={{0,8},{8,16},{16,24},{1,9},{9,17},{17,25},{2,10},{10,18},{18,26},{... | collective-permute-start | bytes 491528 | tf_op jit(solution)/shard_map/ppermute | solution.py:15
  84.6 29.3 %collective-permute-start.14 = (f32[2,40,512]{2,1,0:T(8,128)}, f32[2,40,512]{2,1,0:T(8,128)}, u32[]{:S(2)}, u32[]{:S(2)}) collective-permute-start(f32[2,40,512]{2,1,0:T(8,128)} %get-tuple-element.85), channel_id=1, source_target_pairs={{8,0},{16,8},{24,16},{9,1},{17,9},{25,17},{10,2},{18,10},{26,18},{... | collective-permute-start | bytes 491528 | tf_op jit(solution)/shard_map/ppermute | solution.py:15
  88.5 85.4 %collective-permute-start.12 = (f32[2,160,1]{2,1,0:T(8,128)}, f32[2,160,1]{2,1,0:T(8,128)}, u32[]{:S(2)}, u32[]{:S(2)}) collective-permute-start(f32[2,160,1]{2,1,0:T(8,128)} %get-tuple-element.81), channel_id=1, source_target_pairs={{0,1},{1,2},{2,3},{3,4},{4,5},{5,6},{6,7},{8,9},{9,10},{10,11},{11... | collective-permute-start | bytes 3848 | tf_op jit(solution)/shard_map/ppermute | solution.py:31
  91.3 82.6 %collective-permute-start.13 = (f32[2,160,1]{2,1,0:T(8,128)}, f32[2,160,1]{2,1,0:T(8,128)}, u32[]{:S(2)}, u32[]{:S(2)}) collective-permute-start(f32[2,160,1]{2,1,0:T(8,128)} %get-tuple-element.82), channel_id=1, source_target_pairs={{1,0},{2,1},{3,2},{4,3},{5,4},{6,5},{7,6},{9,8},{10,9},{11,10},{12... | collective-permute-start | bytes 3848 | tf_op jit(solution)/shard_map/ppermute | solution.py:33
  113.7 135.9 %reduce-scatter.27.cloned.1.call-start = ((), (), s32[]{:S(2)}) async-start(), calls=%async_computation.9 | async-start | bytes 1179648
  179.0 15.4 %collective-permute-start.4 = (f32[2,256]{1,0:T(2,128)S(1)}, f32[2,256]{1,0:T(2,128)S(1)}, u32[]{:S(2)}, u32[]{:S(2)}) collective-permute-start(f32[2,256]{1,0:T(2,128)S(1)} %get-tuple-element.123), channel_id=1, source_target_pairs={{0,8},{8,16},{16,24},{1,9},{9,17},{17,25},{2,10},{10,18},{18,26},{... | collective-permute-start | bytes 6152 | tf_op jit(solution)/shard_map/ppermute | solution.py:15
  182.4 31.2 %collective-permute-start.3 = (f32[2,256]{1,0:T(2,128)S(1)}, f32[2,256]{1,0:T(2,128)S(1)}, u32[]{:S(2)}, u32[]{:S(2)}) collective-permute-start(f32[2,256]{1,0:T(2,128)S(1)} %get-tuple-element.122), channel_id=1, source_target_pairs={{8,0},{16,8},{24,16},{9,1},{17,9},{25,17},{10,2},{18,10},{26,18},{... | collective-permute-start | bytes 6152 | tf_op jit(solution)/shard_map/ppermute | solution.py:15
  186.0 119.1 %collective-permute-start.21 = (f32[2,40,512]{2,1,0:T(8,128)}, f32[2,40,512]{2,1,0:T(8,128)}, u32[]{:S(2)}, u32[]{:S(2)}) collective-permute-start(f32[2,40,512]{2,1,0:T(8,128)} %get-tuple-element.77), channel_id=1, source_target_pairs={{0,8},{8,16},{16,24},{1,9},{9,17},{17,25},{2,10},{10,18},{18,26},{... | collective-permute-start | bytes 491528 | tf_op jit(solution)/shard_map/ppermute | solution.py:15
  189.4 117.4 %collective-permute-start.20 = (f32[2,40,512]{2,1,0:T(8,128)}, f32[2,40,512]{2,1,0:T(8,128)}, u32[]{:S(2)}, u32[]{:S(2)}) collective-permute-start(f32[2,40,512]{2,1,0:T(8,128)} %get-tuple-element.76), channel_id=1, source_target_pairs={{8,0},{16,8},{24,16},{9,1},{17,9},{25,17},{10,2},{18,10},{26,18},{... | collective-permute-start | bytes 491528 | tf_op jit(solution)/shard_map/ppermute | solution.py:15
  192.5 116.8 %collective-permute-start.18 = (f32[2,160,1]{2,1,0:T(8,128)}, f32[2,160,1]{2,1,0:T(8,128)}, u32[]{:S(2)}, u32[]{:S(2)}) collective-permute-start(f32[2,160,1]{2,1,0:T(8,128)} %get-tuple-element.72), channel_id=1, source_target_pairs={{0,1},{1,2},{2,3},{3,4},{4,5},{5,6},{6,7},{8,9},{9,10},{10,11},{11... | collective-permute-start | bytes 3848 | tf_op jit(solution)/shard_map/ppermute | solution.py:31
  194.4 114.9 %collective-permute-start.19 = (f32[2,160,1]{2,1,0:T(8,128)}, f32[2,160,1]{2,1,0:T(8,128)}, u32[]{:S(2)}, u32[]{:S(2)}) collective-permute-start(f32[2,160,1]{2,1,0:T(8,128)} %get-tuple-element.73), channel_id=1, source_target_pairs={{1,0},{2,1},{3,2},{4,3},{5,4},{6,5},{7,6},{9,8},{10,9},{11,10},{12... | collective-permute-start | bytes 3848 | tf_op jit(solution)/shard_map/ppermute | solution.py:33
  213.5 119.4 %reduce-scatter.29.cloned.1.call-start = ((), (), s32[]{:S(2)}) async-start(), calls=%async_computation.10 | async-start | bytes 1179648
  263.0 16.5 %collective-permute-start.11 = (f32[2,256]{1,0:T(2,128)S(1)}, f32[2,256]{1,0:T(2,128)S(1)}, u32[]{:S(2)}, u32[]{:S(2)}) collective-permute-start(f32[2,256]{1,0:T(2,128)S(1)} %get-tuple-element.119), channel_id=1, source_target_pairs={{0,8},{8,16},{16,24},{1,9},{9,17},{17,25},{2,10},{10,18},{18,26},{... | collective-permute-start | bytes 6152 | tf_op jit(solution)/shard_map/ppermute | solution.py:15
  279.5 9.3 %collective-permute-start.10 = (f32[2,256]{1,0:T(2,128)S(1)}, f32[2,256]{1,0:T(2,128)S(1)}, u32[]{:S(2)}, u32[]{:S(2)}) collective-permute-start(f32[2,256]{1,0:T(2,128)S(1)} %get-tuple-element.118), channel_id=1, source_target_pairs={{8,0},{16,8},{24,16},{9,1},{17,9},{25,17},{10,2},{18,10},{26,18},{... | collective-permute-start | bytes 6152 | tf_op jit(solution)/shard_map/ppermute | solution.py:15
  296.6 120.0 %reduce-scatter.31.cloned.1.call-start = ((), (), s32[]{:S(2)}) async-start(), calls=%async_computation.11 | async-start | bytes 1179648
  315.8 145.7 %collective-permute-start.27 = (f32[2,40,512]{2,1,0:T(8,128)}, f32[2,40,512]{2,1,0:T(8,128)}, u32[]{:S(2)}, u32[]{:S(2)}) collective-permute-start(f32[2,40,512]{2,1,0:T(8,128)} %get-tuple-element.68), channel_id=1, source_target_pairs={{0,8},{8,16},{16,24},{1,9},{9,17},{17,25},{2,10},{10,18},{18,26},{... | collective-permute-start | bytes 491528 | tf_op jit(solution)/shard_map/ppermute | solution.py:15
  319.2 144.1 %collective-permute-start.26 = (f32[2,40,512]{2,1,0:T(8,128)}, f32[2,40,512]{2,1,0:T(8,128)}, u32[]{:S(2)}, u32[]{:S(2)}) collective-permute-start(f32[2,40,512]{2,1,0:T(8,128)} %get-tuple-element.67), channel_id=1, source_target_pairs={{8,0},{16,8},{24,16},{9,1},{17,9},{25,17},{10,2},{18,10},{26,18},{... | collective-permute-start | bytes 491528 | tf_op jit(solution)/shard_map/ppermute | solution.py:15
  322.3 143.5 %collective-permute-start.24 = (f32[2,160,1]{2,1,0:T(8,128)}, f32[2,160,1]{2,1,0:T(8,128)}, u32[]{:S(2)}, u32[]{:S(2)}) collective-permute-start(f32[2,160,1]{2,1,0:T(8,128)} %get-tuple-element.63), channel_id=1, source_target_pairs={{0,1},{1,2},{2,3},{3,4},{4,5},{5,6},{6,7},{8,9},{9,10},{10,11},{11... | collective-permute-start | bytes 3848 | tf_op jit(solution)/shard_map/ppermute | solution.py:31
  324.2 141.6 %collective-permute-start.25 = (f32[2,160,1]{2,1,0:T(8,128)}, f32[2,160,1]{2,1,0:T(8,128)}, u32[]{:S(2)}, u32[]{:S(2)}) collective-permute-start(f32[2,160,1]{2,1,0:T(8,128)} %get-tuple-element.64), channel_id=1, source_target_pairs={{1,0},{2,1},{3,2},{4,3},{5,4},{6,5},{7,6},{9,8},{10,9},{11,10},{12... | collective-permute-start | bytes 3848 | tf_op jit(solution)/shard_map/ppermute | solution.py:33
  346.3 17.3 %collective-permute-start.17 = (f32[2,256]{1,0:T(2,128)S(1)}, f32[2,256]{1,0:T(2,128)S(1)}, u32[]{:S(2)}, u32[]{:S(2)}) collective-permute-start(f32[2,256]{1,0:T(2,128)S(1)} %get-tuple-element.115), channel_id=1, source_target_pairs={{0,8},{8,16},{16,24},{1,9},{9,17},{17,25},{2,10},{10,18},{18,26},{... | collective-permute-start | bytes 6152 | tf_op jit(solution)/shard_map/ppermute | solution.py:15
  363.6 17.0 %collective-permute-start.16 = (f32[2,256]{1,0:T(2,128)S(1)}, f32[2,256]{1,0:T(2,128)S(1)}, u32[]{:S(2)}, u32[]{:S(2)}) collective-permute-start(f32[2,256]{1,0:T(2,128)S(1)} %get-tuple-element.114), channel_id=1, source_target_pairs={{8,0},{16,8},{24,16},{9,1},{17,9},{25,17},{10,2},{18,10},{26,18},{... | collective-permute-start | bytes 6152 | tf_op jit(solution)/shard_map/ppermute | solution.py:15
  375.9 53.8 %copy-start.52 = (f32[2,4,256]{2,1,0:T(4,128)S(1)}, f32[2,4,256]{2,1,0:T(4,128)}, u32[]{:S(2)}) copy-start(f32[2,4,256]{2,1,0:T(4,128)} %param.10) | copy-start | bytes 24580
  380.5 121.3 %reduce-scatter.33.cloned.1.call-start = ((), (), s32[]{:S(2)}) async-start(), calls=%async_computation.12 | async-start | bytes 1179648
  430.4 5.5 collective-permute-start.23
  435.8 9.0 %collective-permute-start.22 = (f32[2,256]{1,0:T(2,128)}, f32[2,256]{1,0:T(2,128)S(1)}, u32[]{:S(2)}, u32[]{:S(2)}) collective-permute-start(f32[2,256]{1,0:T(2,128)} %get-tuple-element.110), channel_id=1, source_target_pairs={{8,0},{16,8},{24,16},{9,1},{17,9},{25,17},{10,2},{18,10},{26,18},{... | collective-permute-start | bytes 6152 | tf_op jit(solution)/shard_map/ppermute | solution.py:15
  453.1 133.5 %reduce-scatter.35.cloned.1.call-start = ((), (), s32[]{:S(2)}) async-start(), calls=%async_computation.13 | async-start | bytes 1179648
  488.4 57.9 %collective-permute-start.33 = (f32[2,40,512]{2,1,0:T(8,128)}, f32[2,40,512]{2,1,0:T(8,128)}, u32[]{:S(2)}, u32[]{:S(2)}) collective-permute-start(f32[2,40,512]{2,1,0:T(8,128)} %get-tuple-element.59), channel_id=1, source_target_pairs={{0,8},{8,16},{16,24},{1,9},{9,17},{17,25},{2,10},{10,18},{18,26},{... | collective-permute-start | bytes 491528 | tf_op jit(solution)/shard_map/ppermute | solution.py:15
  492.2 55.9 %collective-permute-start.32 = (f32[2,40,512]{2,1,0:T(8,128)}, f32[2,40,512]{2,1,0:T(8,128)}, u32[]{:S(2)}, u32[]{:S(2)}) collective-permute-start(f32[2,40,512]{2,1,0:T(8,128)} %get-tuple-element.58), channel_id=1, source_target_pairs={{8,0},{16,8},{24,16},{9,1},{17,9},{25,17},{10,2},{18,10},{26,18},{... | collective-permute-start | bytes 491528 | tf_op jit(solution)/shard_map/ppermute | solution.py:15
  494.9 55.7 %collective-permute-start.30 = (f32[2,160,1]{2,1,0:T(8,128)}, f32[2,160,1]{2,1,0:T(8,128)}, u32[]{:S(2)}, u32[]{:S(2)}) collective-permute-start(f32[2,160,1]{2,1,0:T(8,128)} %get-tuple-element.54), channel_id=1, source_target_pairs={{0,1},{1,2},{2,3},{3,4},{4,5},{5,6},{6,7},{8,9},{9,10},{10,11},{11... | collective-permute-start | bytes 3848 | tf_op jit(solution)/shard_map/ppermute | solution.py:31
  496.8 53.8 %collective-permute-start.31 = (f32[2,160,1]{2,1,0:T(8,128)}, f32[2,160,1]{2,1,0:T(8,128)}, u32[]{:S(2)}, u32[]{:S(2)}) collective-permute-start(f32[2,160,1]{2,1,0:T(8,128)} %get-tuple-element.55), channel_id=1, source_target_pairs={{1,0},{2,1},{3,2},{4,3},{5,4},{6,5},{7,6},{9,8},{10,9},{11,10},{12... | collective-permute-start | bytes 3848 | tf_op jit(solution)/shard_map/ppermute | solution.py:33
  516.1 5.5 collective-permute-start.29
  521.5 16.6 %collective-permute-start.28 = (f32[2,256]{1,0:T(2,128)}, f32[2,256]{1,0:T(2,128)}, u32[]{:S(2)}, u32[]{:S(2)}) collective-permute-start(f32[2,256]{1,0:T(2,128)} %get-tuple-element.106), channel_id=1, source_target_pairs={{8,0},{16,8},{24,16},{9,1},{17,9},{25,17},{10,2},{18,10},{26,18},{... | collective-permute-start | bytes 6152 | tf_op jit(solution)/shard_map/ppermute | solution.py:15
  538.0 52.5 %copy-start.55 = (f32[4,256]{1,0:T(4,128)S(1)}, f32[4,256]{1,0:T(4,128)}, u32[]{:S(2)}) copy-start(f32[4,256]{1,0:T(4,128)} %copy-done.54) | copy-start | bytes 12292
  538.1 122.0 %reduce-scatter.37.cloned.1.call-start = ((), (), s32[]{:S(2)}) async-start(), calls=%async_computation.14 | async-start | bytes 1179648
  573.7 90.2 %collective-permute-start.39 = (f32[2,40,512]{2,1,0:T(8,128)}, f32[2,40,512]{2,1,0:T(8,128)}, u32[]{:S(2)}, u32[]{:S(2)}) collective-permute-start(f32[2,40,512]{2,1,0:T(8,128)} %get-tuple-element.50), channel_id=1, source_target_pairs={{0,8},{8,16},{16,24},{1,9},{9,17},{17,25},{2,10},{10,18},{18,26},{... | collective-permute-start | bytes 491528 | tf_op jit(solution)/shard_map/ppermute | solution.py:15
  577.5 88.1 %collective-permute-start.38 = (f32[2,40,512]{2,1,0:T(8,128)}, f32[2,40,512]{2,1,0:T(8,128)}, u32[]{:S(2)}, u32[]{:S(2)}) collective-permute-start(f32[2,40,512]{2,1,0:T(8,128)} %get-tuple-element.49), channel_id=1, source_target_pairs={{8,0},{16,8},{24,16},{9,1},{17,9},{25,17},{10,2},{18,10},{26,18},{... | collective-permute-start | bytes 491528 | tf_op jit(solution)/shard_map/ppermute | solution.py:15
  580.2 88.0 %collective-permute-start.36 = (f32[2,160,1]{2,1,0:T(8,128)}, f32[2,160,1]{2,1,0:T(8,128)}, u32[]{:S(2)}, u32[]{:S(2)}) collective-permute-start(f32[2,160,1]{2,1,0:T(8,128)} %get-tuple-element.45), channel_id=1, source_target_pairs={{0,1},{1,2},{2,3},{3,4},{4,5},{5,6},{6,7},{8,9},{9,10},{10,11},{11... | collective-permute-start | bytes 3848 | tf_op jit(solution)/shard_map/ppermute | solution.py:31
  582.1 86.0 %collective-permute-start.37 = (f32[2,160,1]{2,1,0:T(8,128)}, f32[2,160,1]{2,1,0:T(8,128)}, u32[]{:S(2)}, u32[]{:S(2)}) collective-permute-start(f32[2,160,1]{2,1,0:T(8,128)} %get-tuple-element.46), channel_id=1, source_target_pairs={{1,0},{2,1},{3,2},{4,3},{5,4},{6,5},{7,6},{9,8},{10,9},{11,10},{12... | collective-permute-start | bytes 3848 | tf_op jit(solution)/shard_map/ppermute | solution.py:33
  601.0 5.5 collective-permute-start.35
  606.4 16.5 %collective-permute-start.34 = (f32[2,256]{1,0:T(2,128)}, f32[2,256]{1,0:T(2,128)}, u32[]{:S(2)}, u32[]{:S(2)}) collective-permute-start(f32[2,256]{1,0:T(2,128)} %get-tuple-element.102), channel_id=1, source_target_pairs={{8,0},{16,8},{24,16},{9,1},{17,9},{25,17},{10,2},{18,10},{26,18},{... | collective-permute-start | bytes 6152 | tf_op jit(solution)/shard_map/ppermute | solution.py:15
  622.9 149.5 %reduce-scatter.39.cloned.1.call-start = ((), (), s32[]{:S(2)}) async-start(), calls=%async_computation.15 | async-start | bytes 1179648
  701.8 17.3 %collective-permute-start.41 = (f32[2,256]{1,0:T(2,128)S(1)}, f32[2,256]{1,0:T(2,128)S(1)}, u32[]{:S(2)}, u32[]{:S(2)}) collective-permute-start(f32[2,256]{1,0:T(2,128)S(1)} %get-tuple-element.99), channel_id=1, source_target_pairs={{0,8},{8,16},{16,24},{1,9},{9,17},{17,25},{2,10},{10,18},{18,26},{... | collective-permute-start | bytes 6152 | tf_op jit(solution)/shard_map/ppermute | solution.py:15
  706.0 67.8 %collective-permute-start.45 = (f32[2,40,512]{2,1,0:T(8,128)}, f32[2,40,512]{2,1,0:T(8,128)}, u32[]{:S(2)}, u32[]{:S(2)}) collective-permute-start(f32[2,40,512]{2,1,0:T(8,128)} %get-tuple-element.41), channel_id=1, source_target_pairs={{0,8},{8,16},{16,24},{1,9},{9,17},{17,25},{2,10},{10,18},{18,26},{... | collective-permute-start | bytes 491528 | tf_op jit(solution)/shard_map/ppermute | solution.py:15
  709.4 66.2 %collective-permute-start.44 = (f32[2,40,512]{2,1,0:T(8,128)}, f32[2,40,512]{2,1,0:T(8,128)}, u32[]{:S(2)}, u32[]{:S(2)}) collective-permute-start(f32[2,40,512]{2,1,0:T(8,128)} %get-tuple-element.40), channel_id=1, source_target_pairs={{8,0},{16,8},{24,16},{9,1},{17,9},{25,17},{10,2},{18,10},{26,18},{... | collective-permute-start | bytes 491528 | tf_op jit(solution)/shard_map/ppermute | solution.py:15
  712.5 65.6 %collective-permute-start.42 = (f32[2,160,1]{2,1,0:T(8,128)}, f32[2,160,1]{2,1,0:T(8,128)}, u32[]{:S(2)}, u32[]{:S(2)}) collective-permute-start(f32[2,160,1]{2,1,0:T(8,128)} %get-tuple-element.36), channel_id=1, source_target_pairs={{0,1},{1,2},{2,3},{3,4},{4,5},{5,6},{6,7},{8,9},{9,10},{10,11},{11... | collective-permute-start | bytes 3848 | tf_op jit(solution)/shard_map/ppermute | solution.py:31
  714.4 63.6 %collective-permute-start.43 = (f32[2,160,1]{2,1,0:T(8,128)}, f32[2,160,1]{2,1,0:T(8,128)}, u32[]{:S(2)}, u32[]{:S(2)}) collective-permute-start(f32[2,160,1]{2,1,0:T(8,128)} %get-tuple-element.37), channel_id=1, source_target_pairs={{1,0},{2,1},{3,2},{4,3},{5,4},{6,5},{7,6},{9,8},{10,9},{11,10},{12... | collective-permute-start | bytes 3848 | tf_op jit(solution)/shard_map/ppermute | solution.py:33
  719.1 16.8 %collective-permute-start.40 = (f32[2,256]{1,0:T(2,128)}, f32[2,256]{1,0:T(2,128)}, u32[]{:S(2)}, u32[]{:S(2)}) collective-permute-start(f32[2,256]{1,0:T(2,128)} %get-tuple-element.98), channel_id=1, source_target_pairs={{8,0},{16,8},{24,16},{9,1},{17,9},{25,17},{10,2},{18,10},{26,18},{... | collective-permute-start | bytes 6152 | tf_op jit(solution)/shard_map/ppermute | solution.py:15
  728.1 50.0 %copy-start.64 = (f32[160]{0:T(256)S(1)}, f32[160]{0:T(256)}, u32[]{:S(2)}) copy-start(f32[160]{0:T(256)} %get-tuple-element.133) | copy-start | bytes 1924
  728.1 50.0 %copy-start.70 = (f32[2,160]{1,0:T(2,128)S(1)}, f32[2,160]{1,0:T(2,128)}, u32[]{:S(2)}) copy-start(f32[2,160]{1,0:T(2,128)} %get-tuple-element.10) | copy-start | bytes 3844
  781.7 38.5 %collective-permute-start.49 = (f32[2,40,512]{2,1,0:T(8,128)}, f32[2,40,512]{2,1,0:T(8,128)}, u32[]{:S(2)}, u32[]{:S(2)}) collective-permute-start(f32[2,40,512]{2,1,0:T(8,128)} %get-tuple-element.29), channel_id=1, source_target_pairs={{0,8},{8,16},{16,24},{1,9},{9,17},{17,25},{2,10},{10,18},{18,26},{... | collective-permute-start | bytes 491528 | tf_op jit(solution)/shard_map/ppermute | solution.py:15
  785.1 36.7 %collective-permute-start.48 = (f32[2,40,512]{2,1,0:T(8,128)}, f32[2,40,512]{2,1,0:T(8,128)}, u32[]{:S(2)}, u32[]{:S(2)}) collective-permute-start(f32[2,40,512]{2,1,0:T(8,128)} %get-tuple-element.28), channel_id=1, source_target_pairs={{8,0},{16,8},{24,16},{9,1},{17,9},{25,17},{10,2},{18,10},{26,18},{... | collective-permute-start | bytes 491528 | tf_op jit(solution)/shard_map/ppermute | solution.py:15
  789.1 35.0 %collective-permute-start.46 = (f32[2,160,1]{2,1,0:T(8,128)}, f32[2,160,1]{2,1,0:T(8,128)}, u32[]{:S(2)}, u32[]{:S(2)}) collective-permute-start(f32[2,160,1]{2,1,0:T(8,128)} %get-tuple-element.30), channel_id=1, source_target_pairs={{0,1},{1,2},{2,3},{3,4},{4,5},{5,6},{6,7},{8,9},{9,10},{10,11},{11... | collective-permute-start | bytes 3848 | tf_op jit(solution)/shard_map/ppermute | solution.py:31
  791.1 33.1 %collective-permute-start.47 = (f32[2,160,1]{2,1,0:T(8,128)}, f32[2,160,1]{2,1,0:T(8,128)}, u32[]{:S(2)}, u32[]{:S(2)}) collective-permute-start(f32[2,160,1]{2,1,0:T(8,128)} %get-tuple-element.32), channel_id=1, source_target_pairs={{1,0},{2,1},{3,2},{4,3},{5,4},{6,5},{7,6},{9,8},{10,9},{11,10},{12... | collective-permute-start | bytes 3848 | tf_op jit(solution)/shard_map/ppermute | solution.py:33
  (68 other events, 1206.1 us)
Sparse Core Ops, SparseCore 0:
  113.8 34.1 reduce-scatter.24
  213.6 35.9 reduce-scatter.26
  296.7 36.1 reduce-scatter.28
  380.6 35.9 reduce-scatter.30
  453.3 36.6 reduce-scatter.32
  538.2 36.7 reduce-scatter.34
  623.1 36.9 reduce-scatter.36
  736.0 36.3 reduce-scatter.38
where the time goes:
time: 847 us; the launch traced here: 835 us
  matrix products  174 us (21%)
  blocking collectives  169 us (20%)
  starting transfers between devices  156 us (18%)
  waiting for transfers between devices  152 us (18%)
  local copies, waits for them, and re-layouts  136 us (16%)
  other arithmetic  31.5 us (4%)
  between operations  17 us (2%)
    unnamed x16, waiting for transfers between devices  148 us
    ppermute x34, starting transfers between devices, from_behind(): return lax.ppermute(block, axis, route)  103 us
    unnamed x181, local copies, waits for them, and re-layouts  95.9 us
    psum x7, blocking collectives, reduce_partials(): boundary = lax.psum(partial_boundary, 'outer')  92.6 us
    dot_general x8, matrix products, local(): jnp.einsum('lij,plj->pli', dipole, gathered[:, 1:], precision=highest)  79.2 us
    all_gather x8, blocking collectives, local(): gathered = lax.all_gather(extended, 'outer', axis=2, tiled=True)  63.2 us
    dot_general x8, matrix products, local(): jnp.einsum('lji,plj->pli', source_blocks, source_rows, precision=highest)  55.2 us
    ppermute x8, starting transfers between devices, with_halo(): lax.ppermute(head, axis, [((i + 1) % count, i) for i in range(ends)])  36.4 us
  transfers between devices with their start and end apart: 58, of which 9 were waited for; matrix products, arithmetic and copies ran while one was open for 36% of the time, Pallas kernels for 0%

commit v1 on v0

--- a/solution.py
+++ b/solution.py
@@ -39,7 +39,11 @@
 
 def reduce_partials(partial_terms, partial_boundary):
     own_terms = lax.psum_scatter(partial_terms, "outer", scatter_dimension=2, tiled=True)
-    boundary = lax.psum(partial_boundary, "outer")
+    boundary = partial_boundary
+    for hop in (1, 2, 4):
+        boundary = boundary + lax.ppermute(
+            boundary, "outer", [(dev, dev ^ hop) for dev in range(8)]
+        )
     return (own_terms, boundary)
 
 

time: 847 us -> 864 us (1.020)
  waiting for transfers between devices: 152 us -> 195 us
  blocking collectives: 169 us -> 127 us
    psum x7 -> x0, blocking collectives: 92.6 us -> none  [reduce_partials(): boundary = lax.psum(partial_boundary, 'outer')]
    psum x1 -> x4, blocking collectives: 13.1 us -> 53.1 us  [spread(): return lax.psum(jnp.where(mine, shard, jnp.zeros_like(shard)), axis)]
    unnamed x16, waiting for transfers between devices: 148 us -> 171 us
    ppermute x0 -> x24, waiting for transfers between devices: none -> 15.7 us  [reduce_partials(): lax.ppermute(boundary, 'outer', [(dev, dev ^ hop) for dev in range(8)])]
    all_gather x8, blocking collectives: 63.2 us -> 74.1 us  [local(): gathered = lax.all_gather(extended, 'outer', axis=2, tiled=True)]
    unnamed x181 -> x231, local copies, waits for them, and re-layouts: 95.9 us -> 98.9 us
  transfers between devices with their start and end apart: 58 -> 82, of which waited for: 9 -> 14; matrix products, arithmetic and copies ran while one was open for 36% -> 33% of each run, Pallas kernels for 0% -> 0%
where the time goes in v1:
time: 864 us; the launch traced here: 850 us
  waiting for transfers between devices  195 us (23%)
  matrix products  169 us (20%)
  starting transfers between devices  163 us (19%)
  local copies, waits for them, and re-layouts  140 us (16%)
  blocking collectives  127 us (15%)
  other arithmetic  37.5 us (4%)
  between operations  17.4 us (2%)
    unnamed x16, waiting for transfers between devices  171 us
    ppermute x34, starting transfers between devices, from_behind(): return lax.ppermute(block, axis, route)  105 us
    unnamed x231, local copies, waits for them, and re-layouts  98.9 us
    dot_general x8, matrix products, local(): jnp.einsum('lij,plj->pli', dipole, gathered[:, 1:], precision=highest)  81.3 us
    all_gather x8, blocking collectives, local(): gathered = lax.all_gather(extended, 'outer', axis=2, tiled=True)  74.1 us
    psum x4, blocking collectives, spread(): return lax.psum(jnp.where(mine, shard, jnp.zeros_like(shard)), axis)  53.1 us
    dot_general x8, matrix products, local(): jnp.einsum('lji,plj->pli', source_blocks, source_rows, precision=highest)  47.3 us
    ppermute x8, starting transfers between devices, with_halo(): lax.ppermute(head, axis, [((i + 1) % count, i) for i in range(ends)])  34.3 us
  transfers between devices with their start and end apart: 82, of which 14 were waited for; matrix products, arithmetic and copies ran while one was open for 33% of the time, Pallas kernels for 0%

profile of v1, /device:TPU:12, one launch (start us, length us, event | category | flops | bytes accessed | tf_op | source)
XLA Modules:
  0.0 849.6 jit_solution(8659107928719507220)
XLA Ops:
  35.7 6.3 slice.446
  48.0 9.8 %all_gather.24 = f32[2,5,2048]{2,0,1:T(2,128)S(1)} all-gather(f32[2,5,256]{2,0,1:T(2,128)S(1)} %pad_maximum_fusion.23), channel_id=1, replica_groups=mesh['inner'=4,'outer'=8] {'outer'}, dimensions={2}, use_global_device_ids=true | all-gather | bytes 92160 | tf_op jit(solution)/shard_map/all_gather | solution.py:87
  61.2 3.9 collective-permute-start.1
  80.9 12.1 %all-reduce.3 = (f32[2,4,40]{2,0,1:T(2,128)S(1)}, f32[2,4,40]{2,0,1:T(2,128)S(1)}) all-reduce(f32[2,4,40]{2,0,1:T(2,128)S(1)} %copy.69, f32[2,4,40]{2,0,1:T(2,128)S(1)} %copy.79), channel_id=1, replica_groups=mesh['inner'=4,'outer'=8] {'outer'}, use_global_device_ids=true, to_apply=%region_1.2 | all-reduce | flops 640 | bytes 5120 | tf_op jit(solution)/shard_map/psum | solution.py:20
  95.6 4.5 collective-permute-start.20
  102.1 4.5 collective-permute-start.19
  106.6 8.7 %collective-permute-done.2 = f32[256,2048]{1,0:T(8,128)S(1)} collective-permute-done((f32[256,2048]{1,0:T(8,128)}, f32[256,2048]{1,0:T(8,128)S(1)}, u32[]{:S(2)}, u32[]{:S(2)}) %collective-permute-start.2) | collective-permute-done | bytes 2097184 | tf_op jit(solution)/shard_map/ppermute | solution.py:15
  115.4 8.2 convolution_bitcast_fusion.7
  123.6 4.2 copy.137
  127.8 4.5 reshape.173
  135.5 31.8 %reduce-scatter.25.cloned.1.call-done = f32[256,8]{1,0:T(8,128)} async-done(((f32[2048,8]{1,0:T(8,128)}), f32[256,8]{1,0:T(8,128)}) %reduce-scatter.25.cloned.1.call-update) | async-done | bytes 8208
  170.6 10.4 %fusion.55 = f32[2,4,256]{2,0,1:T(2,128)S(1)} fusion(f32[2,4,256]{2,0,1:T(2,128)S(1)} %fusion.63, f32[2,4,256]{2,0,1:T(2,128)S(1)} %copy.138, f32[2,5,2048]{2,0,1:T(2,128)S(1)} %all_gather.24, f32[4,256,2048]{2,1,0:T(8,128)} %param.13, f32[2,4,256]{2,0,1:T(2,128)S(1)} %copy-done.68, f32[]{:T(128)} %bitcast, f32[4,256]{1,0:T(4,128)S(1)} %copy-done.71, ...), kind=kOutput, calls=%fused_computation.81 | convolution fusion | flops 50343936 | bytes 8511492 | tf_op jit(solution)/shard_map/lij,plj->pli/dot_general | solution.py:89
  191.1 4.7 convolution_bitcast_fusion.6
  197.4 8.0 all_gather.25
  205.3 4.2 copy.139
  209.5 4.5 reshape.175
  225.4 25.8 %reduce-scatter.27.cloned.1.call-done = f32[256,8]{1,0:T(8,128)} async-done(((f32[2048,8]{1,0:T(8,128)}), f32[256,8]{1,0:T(8,128)}) %reduce-scatter.27.cloned.1.call-update) | async-done | bytes 8208
  254.3 9.9 %fusion.50 = f32[2,4,256]{2,0,1:T(2,128)S(1)} fusion(f32[2,4,256]{2,0,1:T(2,128)S(1)} %fusion.62, f32[2,4,256]{2,0,1:T(2,128)S(1)} %copy.140, f32[2,5,2048]{2,0,1:T(2,128)S(1)} %all_gather.25, f32[4,256,2048]{2,1,0:T(8,128)} %param.13, f32[4,256]{1,0:T(4,128)S(1)} %get-tuple-element.121, f32[]{:T(128)} %bitcast, f32[4,256]{1,0:T(4,128)S(1)} %compare_convert_fusion, ...), kind=kOutput, calls=%fused_computation.75 | convolution fusion | flops 50345984 | bytes 8511492 | tf_op jit(solution)/shard_map/lij,plj->pli/dot_general | solution.py:89
  271.3 4.1 collective-permute-start.28
  277.9 7.4 convolution_bitcast_fusion.5
  285.4 3.6 collective-permute-done.26
  289.0 9.4 %all_gather.26 = f32[2,5,2048]{2,0,1:T(2,128)S(1)} all-gather(f32[2,5,256]{2,0,1:T(2,128)S(1)} %pad_maximum_fusion.25), channel_id=1, replica_groups=mesh['inner'=4,'outer'=8] {'outer'}, dimensions={2}, use_global_device_ids=true | all-gather | bytes 92160 | tf_op jit(solution)/shard_map/all_gather | solution.py:87
  298.5 4.2 copy.141
  302.6 4.5 reshape.177
  318.5 14.3 %all-reduce.2 = (f32[2,4,40]{2,0,1:T(2,128)S(1)}, f32[2,4,40]{2,0,1:T(2,128)}) all-reduce(f32[2,4,40]{2,0,1:T(2,128)S(1)} %copy.83, f32[2,4,40]{2,0,1:T(2,128)S(1)} %copy.87), channel_id=1, replica_groups=mesh['inner'=4,'outer'=8] {'outer'}, use_global_device_ids=true, to_apply=%region_5.6 | all-reduce | flops 640 | bytes 5120 | tf_op jit(solution)/shard_map/psum | solution.py:20
  333.0 10.4 %reduce-scatter.29.cloned.1.call-done = f32[256,8]{1,0:T(8,128)} async-done(((f32[2048,8]{1,0:T(8,128)}), f32[256,8]{1,0:T(8,128)}) %reduce-scatter.29.cloned.1.call-update) | async-done | bytes 8208
  346.7 10.4 %fusion.45 = f32[2,4,256]{2,0,1:T(2,128)S(1)} fusion(f32[2,4,256]{2,0,1:T(2,128)S(1)} %fusion.61, f32[2,4,256]{2,0,1:T(2,128)S(1)} %copy.142, f32[2,5,2048]{2,0,1:T(2,128)S(1)} %all_gather.26, f32[4,256,2048]{2,1,0:T(8,128)} %param.13, f32[4,256]{1,0:T(4,128)S(1)} %get-tuple-element.122, f32[]{:T(128)} %bitcast, f32[4,256]{1,0:T(4,128)S(1)} %compare_convert_fusion, ...), kind=kOutput, calls=%fused_computation.69 | convolution fusion | flops 50345984 | bytes 8511492 | tf_op jit(solution)/shard_map/lij,plj->pli/dot_general | solution.py:89
  365.8 4.0 convolution_bitcast_fusion.4
  373.0 4.7 reshape.179
  378.4 8.9 %all_gather.27 = f32[2,5,2048]{2,0,1:T(2,128)S(1)} all-gather(f32[2,5,256]{2,0,1:T(2,128)S(1)} %pad_maximum_fusion.26), channel_id=1, replica_groups=mesh['inner'=4,'outer'=8] {'outer'}, dimensions={2}, use_global_device_ids=true | all-gather | bytes 92160 | tf_op jit(solution)/shard_map/all_gather | solution.py:87
  388.5 26.8 %reduce-scatter.31.cloned.1.call-done = f32[256,8]{1,0:T(8,128)} async-done(((f32[2048,8]{1,0:T(8,128)}), f32[256,8]{1,0:T(8,128)}) %reduce-scatter.31.cloned.1.call-update) | async-done | bytes 8208
  418.4 9.9 %fusion.40 = f32[2,4,256]{2,0,1:T(2,128)S(1)} fusion(f32[2,4,256]{2,0,1:T(2,128)} %fusion.60, f32[2,4,256]{2,0,1:T(2,128)S(1)} %copy.144, f32[2,5,2048]{2,0,1:T(2,128)S(1)} %all_gather.27, f32[4,256,2048]{2,1,0:T(8,128)} %param.13, f32[4,256]{1,0:T(4,128)S(1)} %get-tuple-element.120, f32[]{:T(128)} %bitcast, f32[4,256]{1,0:T(4,128)S(1)} %compare_convert_fusion, ...), kind=kOutput, calls=%fused_computation.63 | convolution fusion | flops 50345984 | bytes 8511492 | tf_op jit(solution)/shard_map/lij,plj->pli/dot_general | solution.py:89
  442.7 4.5 collective-permute-start.37
  449.4 7.4 convolution_bitcast_fusion.3
  460.6 9.4 %all_gather.28 = f32[2,5,2048]{2,0,1:T(2,128)S(1)} all-gather(f32[2,5,256]{2,0,1:T(2,128)S(1)} %pad_maximum_fusion.27), channel_id=1, replica_groups=mesh['inner'=4,'outer'=8] {'outer'}, dimensions={2}, use_global_device_ids=true | all-gather | bytes 92160 | tf_op jit(solution)/shard_map/all_gather | solution.py:87
  470.1 4.2 copy.145
  474.3 4.6 reshape.181
  488.8 3.9 collective-permute-start.48
  498.0 4.5 collective-permute-start.46
  503.2 12.7 %reduce-scatter.33.cloned.1.call-done = f32[256,8]{1,0:T(8,128)} async-done(((f32[2048,8]{1,0:T(8,128)}), f32[256,8]{1,0:T(8,128)}) %reduce-scatter.33.cloned.1.call-update) | async-done | bytes 8208
  529.3 13.2 %all-reduce.1 = (f32[2,4,40]{2,0,1:T(2,128)}, f32[2,4,40]{2,0,1:T(2,128)}) all-reduce(f32[2,4,40]{2,0,1:T(2,128)} %copy.91, f32[2,4,40]{2,0,1:T(2,128)} %copy.99), channel_id=1, replica_groups=mesh['inner'=4,'outer'=8] {'outer'}, use_global_device_ids=true, to_apply=%region_9.10 | all-reduce | flops 640 | bytes 5120 | tf_op jit(solution)/shard_map/psum | solution.py:20
  543.6 10.1 %fusion.35 = f32[2,4,256]{2,0,1:T(2,128)S(1)} fusion(f32[2,4,256]{2,0,1:T(2,128)S(1)} %fusion.59, f32[2,4,256]{2,0,1:T(2,128)} %copy.146, f32[2,5,2048]{2,0,1:T(2,128)S(1)} %all_gather.28, f32[4,256,2048]{2,1,0:T(8,128)} %param.13, f32[2,4,256]{2,0,1:T(2,128)S(1)} %fusion.196, f32[]{:T(128)} %bitcast.65, f32[4,256]{1,0:T(4,128)S(1)} %copy-done.71, ...), kind=kOutput, calls=%fused_computation.57 | convolution fusion | flops 50343936 | bytes 8511492 | tf_op jit(solution)/shard_map/lij,plj->pli/dot_general | solution.py:89
  557.0 3.8 collective-permute-start.41
  563.9 4.0 convolution_bitcast_fusion.2
  571.1 4.7 reshape.183
  576.5 9.4 %all_gather.29 = f32[2,5,2048]{2,0,1:T(2,128)S(1)} all-gather(f32[2,5,256]{2,0,1:T(2,128)S(1)} %pad_maximum_fusion.28), channel_id=1, replica_groups=mesh['inner'=4,'outer'=8] {'outer'}, dimensions={2}, use_global_device_ids=true | all-gather | bytes 92160 | tf_op jit(solution)/shard_map/all_gather | solution.py:87
  587.8 25.2 %reduce-scatter.35.cloned.1.call-done = f32[256,8]{1,0:T(8,128)} async-done(((f32[2048,8]{1,0:T(8,128)}), f32[256,8]{1,0:T(8,128)}) %reduce-scatter.35.cloned.1.call-update) | async-done | bytes 8208
  616.8 9.9 %fusion.30 = f32[2,4,256]{2,0,1:T(2,128)S(1)} fusion(f32[2,4,256]{2,0,1:T(2,128)} %fusion.58, f32[2,4,256]{2,0,1:T(2,128)} %copy.148, f32[2,5,2048]{2,0,1:T(2,128)S(1)} %all_gather.29, f32[4,256,2048]{2,1,0:T(8,128)} %param.13, f32[]{:T(128)} %bitcast.65, f32[4,256]{1,0:T(4,128)S(1)} %get-tuple-element.121, f32[4,256]{1,0:T(4,128)S(1)} %compare_convert_fusion, ...), kind=kOutput, calls=%fused_computation.51 | convolution fusion | flops 50345984 | bytes 8511492 | tf_op jit(solution)/shard_map/lij,plj->pli/dot_general | solution.py:89
  641.1 4.5 collective-permute-start.55
  647.7 7.4 convolution_bitcast_fusion.1
  658.9 9.4 %all_gather.30 = f32[2,5,2048]{2,0,1:T(2,128)S(1)} all-gather(f32[2,5,256]{2,0,1:T(2,128)S(1)} %pad_maximum_fusion.29), channel_id=1, replica_groups=mesh['inner'=4,'outer'=8] {'outer'}, dimensions={2}, use_global_device_ids=true | all-gather | bytes 92160 | tf_op jit(solution)/shard_map/all_gather | solution.py:87
  668.3 4.2 copy.149
  672.5 4.5 reshape.185
  685.1 3.9 collective-permute-start.66
  694.3 4.5 collective-permute-start.64
  699.6 14.9 %reduce-scatter.37.cloned.1.call-done = f32[256,8]{1,0:T(8,128)} async-done(((f32[2048,8]{1,0:T(8,128)}), f32[256,8]{1,0:T(8,128)}) %reduce-scatter.37.cloned.1.call-update) | async-done | bytes 8208
  729.1 13.5 %all-reduce = (f32[2,4,40]{2,0,1:T(2,128)}, f32[2,4,40]{2,0,1:T(2,128)}) all-reduce(f32[2,4,40]{2,0,1:T(2,128)} %copy.107, f32[2,4,40]{2,0,1:T(2,128)} %copy.103), channel_id=1, replica_groups=mesh['inner'=4,'outer'=8] {'outer'}, use_global_device_ids=true, to_apply=%region_15.16 | all-reduce | flops 640 | bytes 5120 | tf_op jit(solution)/shard_map/psum | solution.py:20
  743.6 10.1 %fusion.25 = f32[2,4,256]{2,0,1:T(2,128)S(1)} fusion(f32[2,4,256]{2,0,1:T(2,128)S(1)} %fusion.57, f32[2,4,256]{2,0,1:T(2,128)} %copy.150, f32[2,5,2048]{2,0,1:T(2,128)S(1)} %all_gather.30, f32[4,256,2048]{2,1,0:T(8,128)} %param.13, f32[]{:T(128)} %bitcast.65, f32[4,256]{1,0:T(4,128)S(1)} %get-tuple-element.122, f32[4,256]{1,0:T(4,128)S(1)} %compare_convert_fusion, ...), kind=kOutput, calls=%fused_computation.45 | convolution fusion | flops 50345984 | bytes 8511492 | tf_op jit(solution)/shard_map/lij,plj->pli/dot_general | solution.py:89
  766.6 4.3 collective-permute-start.71
  774.0 4.0 convolution_bitcast_fusion
  781.2 4.6 reshape.187
  789.5 9.7 %all_gather.31 = f32[2,5,2048]{2,0,1:T(2,128)S(1)} all-gather(f32[2,5,256]{2,0,1:T(2,128)S(1)} %pad_maximum_fusion.30), channel_id=1, replica_groups=mesh['inner'=4,'outer'=8] {'outer'}, dimensions={2}, use_global_device_ids=true | all-gather | bytes 92160 | tf_op jit(solution)/shard_map/all_gather | solution.py:87
  799.2 23.2 %reduce-scatter.39.cloned.1.call-done = f32[256,8]{1,0:T(8,128)} async-done(((f32[2048,8]{1,0:T(8,128)}), f32[256,8]{1,0:T(8,128)}) %reduce-scatter.39.cloned.1.call-update) | async-done | bytes 8208
  823.9 10.4 %fusion.20 = f32[2,4,256]{2,0,1:T(2,128)S(1)} fusion(f32[2,4,256]{2,0,1:T(2,128)S(1)} %copy-done.76, f32[2,4,256]{2,0,1:T(2,128)S(1)} %copy.152, f32[2,5,2048]{2,0,1:T(2,128)S(1)} %all_gather.31, f32[4,256,2048]{2,1,0:T(8,128)} %param.13, f32[]{:T(128)} %bitcast.65, f32[4,256]{1,0:T(4,128)S(1)} %get-tuple-element.120, ...), kind=kOutput, calls=%fused_computation.39 | convolution fusion | flops 50345984 | bytes 8511492 | tf_op jit(solution)/shard_map/lij,plj->pli/dot_general | solution.py:89
  (574 shorter events, 278.2 us)
Async XLA Ops:
  7.2 160.2 %reduce-scatter.25.cloned.1.call-start = ((), (), s32[]{:S(2)}) async-start(), calls=%async_computation.8 | async-start | bytes 1179648
  9.0 33.2 %collective-permute-start.6 = (f32[2,4,40]{2,0,1:T(2,128)S(1)}, f32[2,4,40]{2,0,1:T(2,128)S(1)}, u32[]{:S(2)}, u32[]{:S(2)}) collective-permute-start(f32[2,4,40]{2,0,1:T(2,128)S(1)} %convolution_bitcast_fusion.23), channel_id=1, source_target_pairs={{0,1},{1,0},{2,3},{3,2},{4,5},{5,4},{6,7},{7,6},{8,9},{9,8},{10,11... | collective-permute-start | bytes 3848 | tf_op jit(solution)/shard_map/ppermute | solution.py:44
  11.0 50.2 %collective-permute-start.12 = (f32[40,40]{0,1:T(8,128)S(1)}, f32[40,40]{0,1:T(8,128)S(1)}, u32[]{:S(2)}, u32[]{:S(2)}) collective-permute-start(f32[40,40]{0,1:T(8,128)S(1)} %slice_bitcast_fusion.17), channel_id=1, source_target_pairs={{0,8},{8,16},{16,24},{1,9},{9,17},{17,25},{2,10},{10,18},{18,26},{... | collective-permute-start | bytes 19208 | tf_op jit(solution)/shard_map/ppermute | solution.py:15
  16.2 49.0 %collective-permute-start.11 = (f32[2,40,512]{2,1,0:T(8,128)S(1)}, f32[2,40,512]{2,1,0:T(8,128)}, u32[]{:S(2)}, u32[]{:S(2)}) collective-permute-start(f32[2,40,512]{2,1,0:T(8,128)S(1)} %get-tuple-element.87), channel_id=1, source_target_pairs={{0,8},{8,16},{16,24},{1,9},{9,17},{17,25},{2,10},{10,18},{18,26},{... | collective-permute-start | bytes 491528 | tf_op jit(solution)/shard_map/ppermute | solution.py:15
  19.7 50.2 %collective-permute-start.10 = (f32[2,40,512]{2,1,0:T(8,128)}, f32[2,40,512]{2,1,0:T(8,128)S(1)}, u32[]{:S(2)}, u32[]{:S(2)}) collective-permute-start(f32[2,40,512]{2,1,0:T(8,128)} %get-tuple-element.86), channel_id=1, source_target_pairs={{8,0},{16,8},{24,16},{9,1},{17,9},{25,17},{10,2},{18,10},{26,18},{... | collective-permute-start | bytes 491528 | tf_op jit(solution)/shard_map/ppermute | solution.py:15
  23.3 20.9 %collective-permute-start = (f32[2,256]{1,0:T(2,128)S(1)}, f32[2,256]{1,0:T(2,128)S(1)}, u32[]{:S(2)}, u32[]{:S(2)}) collective-permute-start(f32[2,256]{1,0:T(2,128)S(1)} %get-tuple-element.118), channel_id=1, source_target_pairs={{8,0},{16,8},{24,16},{9,1},{17,9},{25,17},{10,2},{18,10},{26,18},{... | collective-permute-start | bytes 6152 | tf_op jit(solution)/shard_map/ppermute | solution.py:15
  42.2 30.1 %collective-permute-start.5 = (f32[2,160,1]{2,1,0:T(8,128)}, f32[2,160,1]{2,1,0:T(8,128)S(1)}, u32[]{:S(2)}, u32[]{:S(2)}) collective-permute-start(f32[2,160,1]{2,1,0:T(8,128)} %get-tuple-element.76), channel_id=1, source_target_pairs={{0,1},{1,2},{2,3},{3,4},{4,5},{5,6},{6,7},{8,9},{9,10},{10,11},{11... | collective-permute-start | bytes 3848 | tf_op jit(solution)/shard_map/ppermute | solution.py:31
  47.8 10.0 %collective-permute-start.8 = (f32[2,4,40]{2,0,1:T(2,128)S(1)}, f32[2,4,40]{2,0,1:T(2,128)S(1)}, u32[]{:S(2)}, u32[]{:S(2)}) collective-permute-start(f32[2,4,40]{2,0,1:T(2,128)S(1)} %add.322), channel_id=1, source_target_pairs={{0,4},{1,5},{2,6},{3,7},{4,0},{5,1},{6,2},{7,3},{8,12},{9,13},{10,... | collective-permute-start | bytes 3848 | tf_op jit(solution)/shard_map/ppermute | solution.py:44
  57.8 14.5 %collective-permute-start.9 = (f32[2,160,1]{2,1,0:T(8,128)}, f32[2,160,1]{2,1,0:T(8,128)}, u32[]{:S(2)}, u32[]{:S(2)}) collective-permute-start(f32[2,160,1]{2,1,0:T(8,128)} %get-tuple-element.77), channel_id=1, source_target_pairs={{1,0},{2,1},{3,2},{4,3},{5,4},{6,5},{7,6},{9,8},{10,9},{11,10},{12... | collective-permute-start | bytes 3848 | tf_op jit(solution)/shard_map/ppermute | solution.py:33
  61.2 40.9 %collective-permute-start.1 = (f32[2,256]{1,0:T(2,128)}, f32[2,256]{1,0:T(2,128)S(1)}, u32[]{:S(2)}, u32[]{:S(2)}) collective-permute-start(f32[2,256]{1,0:T(2,128)} %get-tuple-element.119), channel_id=1, source_target_pairs={{0,8},{8,16},{16,24},{1,9},{9,17},{17,25},{2,10},{10,18},{18,26},{... | collective-permute-start | bytes 6152 | tf_op jit(solution)/shard_map/ppermute | solution.py:15
  65.2 50.2 %collective-permute-start.2 = (f32[256,2048]{1,0:T(8,128)}, f32[256,2048]{1,0:T(8,128)S(1)}, u32[]{:S(2)}, u32[]{:S(2)}) collective-permute-start(f32[256,2048]{1,0:T(8,128)} %slice_bitcast_fusion), channel_id=1, source_target_pairs={{0,8},{8,16},{16,24},{1,9},{9,17},{17,25},{2,10},{10,18},{18,26},{... | collective-permute-start | bytes 6291464 | tf_op jit(solution)/shard_map/ppermute | solution.py:15
  79.0 53.9 %collective-permute-start.21 = (f32[2,40,512]{2,1,0:T(8,128)}, f32[2,40,512]{2,1,0:T(8,128)}, u32[]{:S(2)}, u32[]{:S(2)}) collective-permute-start(f32[2,40,512]{2,1,0:T(8,128)} %get-tuple-element.81), channel_id=1, source_target_pairs={{0,8},{8,16},{16,24},{1,9},{9,17},{17,25},{2,10},{10,18},{18,26},{... | collective-permute-start | bytes 491528 | tf_op jit(solution)/shard_map/ppermute | solution.py:15
  95.6 89.2 %collective-permute-start.20 = (f32[2,40,512]{2,1,0:T(8,128)}, f32[2,40,512]{2,1,0:T(8,128)}, u32[]{:S(2)}, u32[]{:S(2)}) collective-permute-start(f32[2,40,512]{2,1,0:T(8,128)} %get-tuple-element.80), channel_id=1, source_target_pairs={{8,0},{16,8},{24,16},{9,1},{17,9},{25,17},{10,2},{18,10},{26,18},{... | collective-permute-start | bytes 491528 | tf_op jit(solution)/shard_map/ppermute | solution.py:15
  100.1 114.3 %collective-permute-start.15 = (f32[2,160,1]{2,1,0:T(8,128)}, f32[2,160,1]{2,1,0:T(8,128)}, u32[]{:S(2)}, u32[]{:S(2)}) collective-permute-start(f32[2,160,1]{2,1,0:T(8,128)} %get-tuple-element.73), channel_id=1, source_target_pairs={{0,1},{1,2},{2,3},{3,4},{4,5},{5,6},{6,7},{8,9},{9,10},{10,11},{11... | collective-permute-start | bytes 3848 | tf_op jit(solution)/shard_map/ppermute | solution.py:31
  102.1 112.3 %collective-permute-start.19 = (f32[2,160,1]{2,1,0:T(8,128)}, f32[2,160,1]{2,1,0:T(8,128)}, u32[]{:S(2)}, u32[]{:S(2)}) collective-permute-start(f32[2,160,1]{2,1,0:T(8,128)} %get-tuple-element.74), channel_id=1, source_target_pairs={{1,0},{2,1},{3,2},{4,3},{5,4},{6,5},{7,6},{9,8},{10,9},{11,10},{12... | collective-permute-start | bytes 3848 | tf_op jit(solution)/shard_map/ppermute | solution.py:33
  132.3 118.8 %reduce-scatter.27.cloned.1.call-start = ((), (), s32[]{:S(2)}) async-start(), calls=%async_computation.9 | async-start | bytes 1179648
  181.1 10.0 %collective-permute-start.4 = (f32[2,256]{1,0:T(2,128)S(1)}, f32[2,256]{1,0:T(2,128)S(1)}, u32[]{:S(2)}, u32[]{:S(2)}) collective-permute-start(f32[2,256]{1,0:T(2,128)S(1)} %get-tuple-element.115), channel_id=1, source_target_pairs={{0,8},{8,16},{16,24},{1,9},{9,17},{17,25},{2,10},{10,18},{18,26},{... | collective-permute-start | bytes 6152 | tf_op jit(solution)/shard_map/ppermute | solution.py:15
  195.8 18.5 %collective-permute-start.18 = (f32[2,4,40]{2,0,1:T(2,128)S(1)}, f32[2,4,40]{2,0,1:T(2,128)S(1)}, u32[]{:S(2)}, u32[]{:S(2)}) collective-permute-start(f32[2,4,40]{2,0,1:T(2,128)S(1)} %add.332), channel_id=1, source_target_pairs={{0,4},{1,5},{2,6},{3,7},{4,0},{5,1},{6,2},{7,3},{8,12},{9,13},{10,... | collective-permute-start | bytes 3848 | tf_op jit(solution)/shard_map/ppermute | solution.py:44
  214.1 129.4 %reduce-scatter.29.cloned.1.call-start = ((), (), s32[]{:S(2)}) async-start(), calls=%async_computation.10 | async-start | bytes 1179648
  218.0 89.6 %collective-permute-start.30 = (f32[2,40,512]{2,1,0:T(8,128)}, f32[2,40,512]{2,1,0:T(8,128)}, u32[]{:S(2)}, u32[]{:S(2)}) collective-permute-start(f32[2,40,512]{2,1,0:T(8,128)} %get-tuple-element.69), channel_id=1, source_target_pairs={{0,8},{8,16},{16,24},{1,9},{9,17},{17,25},{2,10},{10,18},{18,26},{... | collective-permute-start | bytes 491528 | tf_op jit(solution)/shard_map/ppermute | solution.py:15
  221.3 88.0 %collective-permute-start.29 = (f32[2,40,512]{2,1,0:T(8,128)}, f32[2,40,512]{2,1,0:T(8,128)}, u32[]{:S(2)}, u32[]{:S(2)}) collective-permute-start(f32[2,40,512]{2,1,0:T(8,128)} %get-tuple-element.68), channel_id=1, source_target_pairs={{8,0},{16,8},{24,16},{9,1},{17,9},{25,17},{10,2},{18,10},{26,18},{... | collective-permute-start | bytes 491528 | tf_op jit(solution)/shard_map/ppermute | solution.py:15
  264.6 10.8 %collective-permute-start.14 = (f32[2,256]{1,0:T(2,128)S(1)}, f32[2,256]{1,0:T(2,128)S(1)}, u32[]{:S(2)}, u32[]{:S(2)}) collective-permute-start(f32[2,256]{1,0:T(2,128)S(1)} %get-tuple-element.111), channel_id=1, source_target_pairs={{0,8},{8,16},{16,24},{1,9},{9,17},{17,25},{2,10},{10,18},{18,26},{... | collective-permute-start | bytes 6152 | tf_op jit(solution)/shard_map/ppermute | solution.py:15
  268.8 43.0 %collective-permute-start.24 = (f32[2,160,1]{2,1,0:T(8,128)}, f32[2,160,1]{2,1,0:T(8,128)}, u32[]{:S(2)}, u32[]{:S(2)}) collective-permute-start(f32[2,160,1]{2,1,0:T(8,128)} %get-tuple-element.58), channel_id=1, source_target_pairs={{0,1},{1,2},{2,3},{3,4},{4,5},{5,6},{6,7},{8,9},{9,10},{10,11},{11... | collective-permute-start | bytes 3848 | tf_op jit(solution)/shard_map/ppermute | solution.py:31
  271.3 40.6 %collective-permute-start.28 = (f32[2,160,1]{2,1,0:T(8,128)}, f32[2,160,1]{2,1,0:T(8,128)}, u32[]{:S(2)}, u32[]{:S(2)}) collective-permute-start(f32[2,160,1]{2,1,0:T(8,128)} %get-tuple-element.59), channel_id=1, source_target_pairs={{1,0},{2,1},{3,2},{4,3},{5,4},{6,5},{7,6},{9,8},{10,9},{11,10},{12... | collective-permute-start | bytes 3848 | tf_op jit(solution)/shard_map/ppermute | solution.py:33
  289.0 18.4 %collective-permute-start.27 = (f32[2,4,40]{2,0,1:T(2,128)S(1)}, f32[2,4,40]{2,0,1:T(2,128)S(1)}, u32[]{:S(2)}, u32[]{:S(2)}) collective-permute-start(f32[2,4,40]{2,0,1:T(2,128)S(1)} %add.342), channel_id=1, source_target_pairs={{0,4},{1,5},{2,6},{3,7},{4,0},{5,1},{6,2},{7,3},{8,12},{9,13},{10,... | collective-permute-start | bytes 3848 | tf_op jit(solution)/shard_map/ppermute | solution.py:44
  307.2 108.0 %reduce-scatter.31.cloned.1.call-start = ((), (), s32[]{:S(2)}) async-start(), calls=%async_computation.11 | async-start | bytes 1179648
  362.3 15.5 %collective-permute-start.22 = (f32[2,256]{1,0:T(2,128)}, f32[2,256]{1,0:T(2,128)}, u32[]{:S(2)}, u32[]{:S(2)}) collective-permute-start(f32[2,256]{1,0:T(2,128)} %get-tuple-element.106), channel_id=1, source_target_pairs={{8,0},{16,8},{24,16},{9,1},{17,9},{25,17},{10,2},{18,10},{26,18},{... | collective-permute-start | bytes 6152 | tf_op jit(solution)/shard_map/ppermute | solution.py:15
  365.1 22.2 %collective-permute-start.35 = (f32[2,4,40]{2,0,1:T(2,128)S(1)}, f32[2,4,40]{2,0,1:T(2,128)S(1)}, u32[]{:S(2)}, u32[]{:S(2)}) collective-permute-start(f32[2,4,40]{2,0,1:T(2,128)S(1)} %add.354), channel_id=1, source_target_pairs={{0,2},{1,3},{2,0},{3,1},{4,6},{5,7},{6,4},{7,5},{8,10},{9,11},{10,... | collective-permute-start | bytes 3848 | tf_op jit(solution)/shard_map/ppermute | solution.py:44
  377.7 138.3 %reduce-scatter.33.cloned.1.call-start = ((), (), s32[]{:S(2)}) async-start(), calls=%async_computation.12 | async-start | bytes 1179648
  387.9 51.5 %collective-permute-start.36 = (f32[2,4,40]{2,0,1:T(2,128)}, f32[2,4,40]{2,0,1:T(2,128)}, u32[]{:S(2)}, u32[]{:S(2)}) collective-permute-start(f32[2,4,40]{2,0,1:T(2,128)} %add.355), channel_id=1, source_target_pairs={{0,4},{1,5},{2,6},{3,7},{4,0},{5,1},{6,2},{7,3},{8,12},{9,13},{10,... | collective-permute-start | bytes 3848 | tf_op jit(solution)/shard_map/ppermute | solution.py:44
  428.7 18.6 %collective-permute-start.32 = (f32[2,256]{1,0:T(2,128)S(1)}, f32[2,256]{1,0:T(2,128)S(1)}, u32[]{:S(2)}, u32[]{:S(2)}) collective-permute-start(f32[2,256]{1,0:T(2,128)S(1)} %get-tuple-element.103), channel_id=1, source_target_pairs={{0,8},{8,16},{16,24},{1,9},{9,17},{17,25},{2,10},{10,18},{18,26},{... | collective-permute-start | bytes 6152 | tf_op jit(solution)/shard_map/ppermute | solution.py:15
  432.1 10.6 %collective-permute-start.43 = (f32[2,4,40]{2,0,1:T(2,128)S(1)}, f32[2,4,40]{2,0,1:T(2,128)S(1)}, u32[]{:S(2)}, u32[]{:S(2)}) collective-permute-start(f32[2,4,40]{2,0,1:T(2,128)S(1)} %convolution_bitcast_fusion.19), channel_id=1, source_target_pairs={{0,1},{1,0},{2,3},{3,2},{4,5},{5,4},{6,7},{7,6},{8,9},{9,8},{10,11... | collective-permute-start | bytes 3848 | tf_op jit(solution)/shard_map/ppermute | solution.py:44
  433.0 46.1 %collective-permute-start.39 = (f32[2,40,512]{2,1,0:T(8,128)}, f32[2,40,512]{2,1,0:T(8,128)}, u32[]{:S(2)}, u32[]{:S(2)}) collective-permute-start(f32[2,40,512]{2,1,0:T(8,128)} %get-tuple-element.63), channel_id=1, source_target_pairs={{0,8},{8,16},{16,24},{1,9},{9,17},{17,25},{2,10},{10,18},{18,26},{... | collective-permute-start | bytes 491528 | tf_op jit(solution)/shard_map/ppermute | solution.py:15
  436.3 44.5 %collective-permute-start.38 = (f32[2,40,512]{2,1,0:T(8,128)}, f32[2,40,512]{2,1,0:T(8,128)}, u32[]{:S(2)}, u32[]{:S(2)}) collective-permute-start(f32[2,40,512]{2,1,0:T(8,128)} %get-tuple-element.62), channel_id=1, source_target_pairs={{8,0},{16,8},{24,16},{9,1},{17,9},{25,17},{10,2},{18,10},{26,18},{... | collective-permute-start | bytes 491528 | tf_op jit(solution)/shard_map/ppermute | solution.py:15
  439.5 43.9 %collective-permute-start.33 = (f32[2,160,1]{2,1,0:T(8,128)}, f32[2,160,1]{2,1,0:T(8,128)}, u32[]{:S(2)}, u32[]{:S(2)}) collective-permute-start(f32[2,160,1]{2,1,0:T(8,128)} %get-tuple-element.55), channel_id=1, source_target_pairs={{0,1},{1,2},{2,3},{3,4},{4,5},{5,6},{6,7},{8,9},{9,10},{10,11},{11... | collective-permute-start | bytes 3848 | tf_op jit(solution)/shard_map/ppermute | solution.py:31
  442.7 40.6 %collective-permute-start.37 = (f32[2,160,1]{2,1,0:T(8,128)}, f32[2,160,1]{2,1,0:T(8,128)}, u32[]{:S(2)}, u32[]{:S(2)}) collective-permute-start(f32[2,160,1]{2,1,0:T(8,128)} %get-tuple-element.56), channel_id=1, source_target_pairs={{1,0},{2,1},{3,2},{4,3},{5,4},{6,5},{7,6},{9,8},{10,9},{11,10},{12... | collective-permute-start | bytes 3848 | tf_op jit(solution)/shard_map/ppermute | solution.py:33
  460.6 18.4 %collective-permute-start.45 = (f32[2,4,40]{2,0,1:T(2,128)S(1)}, f32[2,4,40]{2,0,1:T(2,128)S(1)}, u32[]{:S(2)}, u32[]{:S(2)}) collective-permute-start(f32[2,4,40]{2,0,1:T(2,128)S(1)} %add.366), channel_id=1, source_target_pairs={{0,4},{1,5},{2,6},{3,7},{4,0},{5,1},{6,2},{7,3},{8,12},{9,13},{10,... | collective-permute-start | bytes 3848 | tf_op jit(solution)/shard_map/ppermute | solution.py:44
  478.9 134.1 %reduce-scatter.35.cloned.1.call-start = ((), (), s32[]{:S(2)}) async-start(), calls=%async_computation.13 | async-start | bytes 1179648
  488.8 29.1 %collective-permute-start.48 = (f32[2,40,512]{2,1,0:T(8,128)}, f32[2,40,512]{2,1,0:T(8,128)}, u32[]{:S(2)}, u32[]{:S(2)}) collective-permute-start(f32[2,40,512]{2,1,0:T(8,128)} %get-tuple-element.51), channel_id=1, source_target_pairs={{0,8},{8,16},{16,24},{1,9},{9,17},{17,25},{2,10},{10,18},{18,26},{... | collective-permute-start | bytes 491528 | tf_op jit(solution)/shard_map/ppermute | solution.py:15
  493.5 26.1 %collective-permute-start.47 = (f32[2,40,512]{2,1,0:T(8,128)}, f32[2,40,512]{2,1,0:T(8,128)S(1)}, u32[]{:S(2)}, u32[]{:S(2)}) collective-permute-start(f32[2,40,512]{2,1,0:T(8,128)} %get-tuple-element.50), channel_id=1, source_target_pairs={{8,0},{16,8},{24,16},{9,1},{17,9},{25,17},{10,2},{18,10},{26,18},{... | collective-permute-start | bytes 491528 | tf_op jit(solution)/shard_map/ppermute | solution.py:15
  496.1 26.7 %collective-permute-start.42 = (f32[2,160,1]{2,1,0:T(8,128)}, f32[2,160,1]{2,1,0:T(8,128)}, u32[]{:S(2)}, u32[]{:S(2)}) collective-permute-start(f32[2,160,1]{2,1,0:T(8,128)} %get-tuple-element.40), channel_id=1, source_target_pairs={{0,1},{1,2},{2,3},{3,4},{4,5},{5,6},{6,7},{8,9},{9,10},{10,11},{11... | collective-permute-start | bytes 3848 | tf_op jit(solution)/shard_map/ppermute | solution.py:31
  498.0 24.8 %collective-permute-start.46 = (f32[2,160,1]{2,1,0:T(8,128)}, f32[2,160,1]{2,1,0:T(8,128)}, u32[]{:S(2)}, u32[]{:S(2)}) collective-permute-start(f32[2,160,1]{2,1,0:T(8,128)} %get-tuple-element.41), channel_id=1, source_target_pairs={{1,0},{2,1},{3,2},{4,3},{5,4},{6,5},{7,6},{9,8},{10,9},{11,10},{12... | collective-permute-start | bytes 3848 | tf_op jit(solution)/shard_map/ppermute | solution.py:33
  554.6 21.3 %collective-permute-start.40 = (f32[2,256]{1,0:T(2,128)}, f32[2,256]{1,0:T(2,128)}, u32[]{:S(2)}, u32[]{:S(2)}) collective-permute-start(f32[2,256]{1,0:T(2,128)} %get-tuple-element.98), channel_id=1, source_target_pairs={{8,0},{16,8},{24,16},{9,1},{17,9},{25,17},{10,2},{18,10},{26,18},{... | collective-permute-start | bytes 6152 | tf_op jit(solution)/shard_map/ppermute | solution.py:15
  563.8 22.2 %collective-permute-start.53 = (f32[2,4,40]{2,0,1:T(2,128)S(1)}, f32[2,4,40]{2,0,1:T(2,128)}, u32[]{:S(2)}, u32[]{:S(2)}) collective-permute-start(f32[2,4,40]{2,0,1:T(2,128)S(1)} %add.375), channel_id=1, source_target_pairs={{0,2},{1,3},{2,0},{3,1},{4,6},{5,7},{6,4},{7,5},{8,10},{9,11},{10,... | collective-permute-start | bytes 3848 | tf_op jit(solution)/shard_map/ppermute | solution.py:44
  575.8 138.7 %reduce-scatter.37.cloned.1.call-start = ((), (), s32[]{:S(2)}) async-start(), calls=%async_computation.14 | async-start | bytes 1179648
  587.2 50.5 %collective-permute-start.54 = (f32[2,4,40]{2,0,1:T(2,128)}, f32[2,4,40]{2,0,1:T(2,128)}, u32[]{:S(2)}, u32[]{:S(2)}) collective-permute-start(f32[2,4,40]{2,0,1:T(2,128)} %add.376), channel_id=1, source_target_pairs={{0,4},{1,5},{2,6},{3,7},{4,0},{5,1},{6,2},{7,3},{8,12},{9,13},{10,... | collective-permute-start | bytes 3848 | tf_op jit(solution)/shard_map/ppermute | solution.py:44
  627.0 18.6 %collective-permute-start.50 = (f32[2,256]{1,0:T(2,128)S(1)}, f32[2,256]{1,0:T(2,128)S(1)}, u32[]{:S(2)}, u32[]{:S(2)}) collective-permute-start(f32[2,256]{1,0:T(2,128)S(1)} %get-tuple-element.95), channel_id=1, source_target_pairs={{0,8},{8,16},{16,24},{1,9},{9,17},{17,25},{2,10},{10,18},{18,26},{... | collective-permute-start | bytes 6152 | tf_op jit(solution)/shard_map/ppermute | solution.py:15
  630.4 10.6 %collective-permute-start.61 = (f32[2,4,40]{2,0,1:T(2,128)S(1)}, f32[2,4,40]{2,0,1:T(2,128)S(1)}, u32[]{:S(2)}, u32[]{:S(2)}) collective-permute-start(f32[2,4,40]{2,0,1:T(2,128)S(1)} %convolution_bitcast_fusion.17), channel_id=1, source_target_pairs={{0,1},{1,0},{2,3},{3,2},{4,5},{5,4},{6,7},{7,6},{8,9},{9,8},{10,11... | collective-permute-start | bytes 3848 | tf_op jit(solution)/shard_map/ppermute | solution.py:44
  631.3 46.0 %collective-permute-start.57 = (f32[2,40,512]{2,1,0:T(8,128)}, f32[2,40,512]{2,1,0:T(8,128)}, u32[]{:S(2)}, u32[]{:S(2)}) collective-permute-start(f32[2,40,512]{2,1,0:T(8,128)} %get-tuple-element.45), channel_id=1, source_target_pairs={{0,8},{8,16},{16,24},{1,9},{9,17},{17,25},{2,10},{10,18},{18,26},{... | collective-permute-start | bytes 491528 | tf_op jit(solution)/shard_map/ppermute | solution.py:15
  634.7 44.3 %collective-permute-start.56 = (f32[2,40,512]{2,1,0:T(8,128)}, f32[2,40,512]{2,1,0:T(8,128)}, u32[]{:S(2)}, u32[]{:S(2)}) collective-permute-start(f32[2,40,512]{2,1,0:T(8,128)} %get-tuple-element.44), channel_id=1, source_target_pairs={{8,0},{16,8},{24,16},{9,1},{17,9},{25,17},{10,2},{18,10},{26,18},{... | collective-permute-start | bytes 491528 | tf_op jit(solution)/shard_map/ppermute | solution.py:15
  637.8 43.8 %collective-permute-start.51 = (f32[2,160,1]{2,1,0:T(8,128)}, f32[2,160,1]{2,1,0:T(8,128)}, u32[]{:S(2)}, u32[]{:S(2)}) collective-permute-start(f32[2,160,1]{2,1,0:T(8,128)} %get-tuple-element.37), channel_id=1, source_target_pairs={{0,1},{1,2},{2,3},{3,4},{4,5},{5,6},{6,7},{8,9},{9,10},{10,11},{11... | collective-permute-start | bytes 3848 | tf_op jit(solution)/shard_map/ppermute | solution.py:31
  641.1 40.5 %collective-permute-start.55 = (f32[2,160,1]{2,1,0:T(8,128)}, f32[2,160,1]{2,1,0:T(8,128)}, u32[]{:S(2)}, u32[]{:S(2)}) collective-permute-start(f32[2,160,1]{2,1,0:T(8,128)} %get-tuple-element.38), channel_id=1, source_target_pairs={{1,0},{2,1},{3,2},{4,3},{5,4},{6,5},{7,6},{9,8},{10,9},{11,10},{12... | collective-permute-start | bytes 3848 | tf_op jit(solution)/shard_map/ppermute | solution.py:33
  658.9 18.2 %collective-permute-start.63 = (f32[2,4,40]{2,0,1:T(2,128)S(1)}, f32[2,4,40]{2,0,1:T(2,128)S(1)}, u32[]{:S(2)}, u32[]{:S(2)}) collective-permute-start(f32[2,4,40]{2,0,1:T(2,128)S(1)} %add.386), channel_id=1, source_target_pairs={{0,4},{1,5},{2,6},{3,7},{4,0},{5,1},{6,2},{7,3},{8,12},{9,13},{10,... | collective-permute-start | bytes 3848 | tf_op jit(solution)/shard_map/ppermute | solution.py:44
  677.1 145.4 %reduce-scatter.39.cloned.1.call-start = ((), (), s32[]{:S(2)}) async-start(), calls=%async_computation.15 | async-start | bytes 1179648
  685.1 31.3 %collective-permute-start.66 = (f32[2,40,512]{2,1,0:T(8,128)S(1)}, f32[2,40,512]{2,1,0:T(8,128)}, u32[]{:S(2)}, u32[]{:S(2)}) collective-permute-start(f32[2,40,512]{2,1,0:T(8,128)S(1)} %get-tuple-element.33), channel_id=1, source_target_pairs={{0,8},{8,16},{16,24},{1,9},{9,17},{17,25},{2,10},{10,18},{18,26},{... | collective-permute-start | bytes 491528 | tf_op jit(solution)/shard_map/ppermute | solution.py:15
  689.1 29.1 %collective-permute-start.65 = (f32[2,40,512]{2,1,0:T(8,128)}, f32[2,40,512]{2,1,0:T(8,128)}, u32[]{:S(2)}, u32[]{:S(2)}) collective-permute-start(f32[2,40,512]{2,1,0:T(8,128)} %get-tuple-element.32), channel_id=1, source_target_pairs={{8,0},{16,8},{24,16},{9,1},{17,9},{25,17},{10,2},{18,10},{26,18},{... | collective-permute-start | bytes 491528 | tf_op jit(solution)/shard_map/ppermute | solution.py:15
  692.4 28.3 %collective-permute-start.60 = (f32[2,160,1]{2,1,0:T(8,128)}, f32[2,160,1]{2,1,0:T(8,128)}, u32[]{:S(2)}, u32[]{:S(2)}) collective-permute-start(f32[2,160,1]{2,1,0:T(8,128)} %get-tuple-element.26), channel_id=1, source_target_pairs={{0,1},{1,2},{2,3},{3,4},{4,5},{5,6},{6,7},{8,9},{9,10},{10,11},{11... | collective-permute-start | bytes 3848 | tf_op jit(solution)/shard_map/ppermute | solution.py:31
  694.3 26.4 %collective-permute-start.64 = (f32[2,160,1]{2,1,0:T(8,128)}, f32[2,160,1]{2,1,0:T(8,128)}, u32[]{:S(2)}, u32[]{:S(2)}) collective-permute-start(f32[2,160,1]{2,1,0:T(8,128)} %get-tuple-element.27), channel_id=1, source_target_pairs={{1,0},{2,1},{3,2},{4,3},{5,4},{6,5},{7,6},{9,8},{10,9},{11,10},{12... | collective-permute-start | bytes 3848 | tf_op jit(solution)/shard_map/ppermute | solution.py:33
  754.6 12.0 %collective-permute-start.68 = (f32[2,4,40]{2,0,1:T(2,128)S(1)}, f32[2,4,40]{2,0,1:T(2,128)S(1)}, u32[]{:S(2)}, u32[]{:S(2)}) collective-permute-start(f32[2,4,40]{2,0,1:T(2,128)S(1)} %convolution_bitcast_fusion.16), channel_id=1, source_target_pairs={{0,1},{1,0},{2,3},{3,2},{4,5},{5,4},{6,7},{7,6},{8,9},{9,8},{10,11... | collective-permute-start | bytes 3848 | tf_op jit(solution)/shard_map/ppermute | solution.py:44
  754.6 80.5 %collective-permute-start.73 = (f32[2,40,512]{2,1,0:T(8,128)}, f32[2,40,512]{2,1,0:T(8,128)}, u32[]{:S(2)}, u32[]{:S(2)}) collective-permute-start(f32[2,40,512]{2,1,0:T(8,128)} %get-tuple-element.21), channel_id=1, source_target_pairs={{0,8},{8,16},{16,24},{1,9},{9,17},{17,25},{2,10},{10,18},{18,26},{... | collective-permute-start | bytes 491528 | tf_op jit(solution)/shard_map/ppermute | solution.py:15
  758.0 78.7 %collective-permute-start.72 = (f32[2,40,512]{2,1,0:T(8,128)}, f32[2,40,512]{2,1,0:T(8,128)}, u32[]{:S(2)}, u32[]{:S(2)}) collective-permute-start(f32[2,40,512]{2,1,0:T(8,128)} %get-tuple-element.20), channel_id=1, source_target_pairs={{8,0},{16,8},{24,16},{9,1},{17,9},{25,17},{10,2},{18,10},{26,18},{... | collective-permute-start | bytes 491528 | tf_op jit(solution)/shard_map/ppermute | solution.py:15
  761.1 78.0 %collective-permute-start.67 = (f32[2,160,1]{2,1,0:T(8,128)}, f32[2,160,1]{2,1,0:T(8,128)}, u32[]{:S(2)}, u32[]{:S(2)}) collective-permute-start(f32[2,160,1]{2,1,0:T(8,128)} %get-tuple-element.22), channel_id=1, source_target_pairs={{0,1},{1,2},{2,3},{3,4},{4,5},{5,6},{6,7},{8,9},{9,10},{10,11},{11... | collective-permute-start | bytes 3848 | tf_op jit(solution)/shard_map/ppermute | solution.py:31
  766.6 72.5 %collective-permute-start.71 = (f32[2,160,1]{2,1,0:T(8,128)}, f32[2,160,1]{2,1,0:T(8,128)}, u32[]{:S(2)}, u32[]{:S(2)}) collective-permute-start(f32[2,160,1]{2,1,0:T(8,128)} %get-tuple-element.24), channel_id=1, source_target_pairs={{1,0},{2,1},{3,2},{4,3},{5,4},{6,5},{7,6},{9,8},{10,9},{11,10},{12... | collective-permute-start | bytes 3848 | tf_op jit(solution)/shard_map/ppermute | solution.py:33
  770.9 14.9 %collective-permute-start.58 = (f32[2,256]{1,0:T(2,128)}, f32[2,256]{1,0:T(2,128)}, u32[]{:S(2)}, u32[]{:S(2)}) collective-permute-start(f32[2,256]{1,0:T(2,128)} %get-tuple-element.90), channel_id=1, source_target_pairs={{8,0},{16,8},{24,16},{9,1},{17,9},{25,17},{10,2},{18,10},{26,18},{... | collective-permute-start | bytes 6152 | tf_op jit(solution)/shard_map/ppermute | solution.py:15
  (117 other events, 2502.5 us)
Sparse Core Ops, SparseCore 0:
  132.5 34.8 reduce-scatter.24
  214.2 36.9 reduce-scatter.26
  307.3 36.0 reduce-scatter.28
  377.8 37.3 reduce-scatter.30
  479.0 36.8 reduce-scatter.32
  575.9 37.0 reduce-scatter.34
  677.2 37.2 reduce-scatter.36
  785.9 36.4 reduce-scatter.38
